TPU v7x, 32 devices: a whole 2x2x4 slice. The times are simulated.
32 devices in a mesh: rows: 8 (over z, y), pairs: 4 (over x, core).
Axes of the slice: x: 2, y: 2, z: 4, core: 2. Of those that a mesh axis runs over, the one named last changes fastest.
Arguments:
- matrix: float32 [16384, 2048], P('rows', 'pairs'), may hold values from -40 to 40
Outputs:
- rotated: float32 [16384, 2048], P('rows', 'pairs')
All inputs are finite; a program needn't handle non-finite values.
Results may differ from a plain program's by a relative error of at most 0.0001.
Values sent between devices are 32-bit elements; how exact they have to be, the bound alone decides.
A program may use at most 64 MiB of HBM per device.

v0:
```python
import functools

import jax
import jax.numpy as jnp
from jax import lax
from jax.experimental import pallas as pl
from jax.experimental.pallas import tpu as pltpu
from jax.sharding import PartitionSpec as P

STEPS = 2
CHUNKS = 8
F32 = jnp.float32
BF16 = jnp.bfloat16
MESH = pl.DeviceIdType.MESH


def split(value):
    high = value.astype(BF16)
    return high, (value - high.astype(F32)).astype(BF16)


def dot_bf16(left, right, left_dim):
    return lax.dot_general(
        left, right, (((left_dim,), (0,)), ((), ())), preferred_element_type=F32
    )


def dot_three(left, right, left_dim):
    return (
        dot_bf16(left[0], right[1], left_dim)
        + dot_bf16(left[1], right[0], left_dim)
        + dot_bf16(left[0], right[0], left_dim)
    )


def exact_dot(left, right, left_dim=1):
    return lax.dot_general(
        left,
        right,
        (((left_dim,), (0,)), ((), ())),
        precision=lax.Precision.HIGHEST,
        preferred_element_type=F32,
    )


def sum_over_rows(count, part, total, recv, mine, gathered, sems):
    send_one, recv_one, send_two, recv_two = sems
    me = lax.axis_index("rows")
    first_copies = []
    for far in range(1, count):
        peer = lax.rem(me + far, count)
        copy = pltpu.make_async_remote_copy(
            src_ref=part.at[peer],
            dst_ref=recv.at[far],
            send_sem=send_one.at[far],
            recv_sem=recv_one.at[far],
            device_id={"rows": peer},
            device_id_type=MESH,
        )
        copy.start()
        first_copies.append(copy)
    acc = part[me]
    for far in range(1, count):
        first_copies[far - 1].wait_recv()
        acc = acc + recv[far]
    mine[...] = acc
    second_copies = []
    for far in range(1, count):
        peer = lax.rem(me + far, count)
        copy = pltpu.make_async_remote_copy(
            src_ref=mine,
            dst_ref=gathered.at[far],
            send_sem=send_two.at[far],
            recv_sem=recv_two.at[far],
            device_id={"rows": peer},
            device_id_type=MESH,
        )
        copy.start()
        second_copies.append(copy)
    total[me] = acc
    for far in range(1, count):
        second_copies[far - 1].wait_recv()
        total[lax.rem(me + count - far, count)] = gathered[far]
    for copy in first_copies + second_copies:
        copy.wait_send()


def stage_kernel(rotates, sums, count, length, *refs):
    refs = list(refs)
    matrix = refs.pop(0)
    if rotates:
        rot_high, rot_low = refs.pop(0), refs.pop(0)
        moved = refs.pop(0)
    if sums:
        total = refs.pop(0)
    loaded, load_sem = refs.pop(0), refs.pop(0)
    if rotates:
        up, other, land_first, land_second = (refs.pop(0) for _ in range(4))
        up_send, up_recv, down_send, down_recv, store_sem = (refs.pop(0) for _ in range(5))
    if sums:
        cross, norms, part, recv, mine, gathered = (refs.pop(0) for _ in range(6))
        sums_sems = tuple(refs.pop(0) for _ in range(4))
    rows, cols = loaded.shape
    block = cols // 2
    step = rows // CHUNKS
    position = lax.axis_index("pairs")
    lowest = position == 0
    highest = position == length - 1

    def at(chunk):
        return pl.ds(pl.multiple_of(chunk * step, step), step)

    def load(chunk):
        return pltpu.make_async_copy(
            matrix.at[at(chunk)], loaded.at[at(chunk)], load_sem.at[chunk]
        )

    def to_upper(chunk):
        return pltpu.make_async_remote_copy(
            src_ref=up.at[at(chunk)],
            dst_ref=land_first.at[at(chunk)],
            send_sem=up_send.at[chunk],
            recv_sem=up_recv.at[chunk],
            device_id={"pairs": lax.rem(position + 1, length)},
            device_id_type=MESH,
        )

    def to_lower(chunk):
        return pltpu.make_async_remote_copy(
            src_ref=other.at[at(chunk)],
            dst_ref=land_second.at[at(chunk)],
            send_sem=down_send.at[chunk],
            recv_sem=down_recv.at[chunk],
            device_id={"pairs": lax.rem(position + length - 1, length)},
            device_id_type=MESH,
        )

    def store(chunk, half):
        source = land_second if half else land_first
        return pltpu.make_async_copy(
            source.at[at(chunk)],
            moved.at[at(chunk), pl.ds(half * block, block)],
            store_sem.at[half, chunk],
        )

    for chunk in range(CHUNKS):
        load(chunk).start()

    barrier = pltpu.get_barrier_semaphore()
    if sums:
        me = lax.axis_index("rows")
        for far in range(1, count):
            pl.semaphore_signal(
                barrier,
                inc=1,
                device_id={"rows": lax.rem(me + far, count)},
                device_id_type=MESH,
            )
    greeted = jnp.int32(count - 1 if sums else 0)
    if rotates:
        @pl.when(jnp.logical_not(lowest))
        def _():
            pl.semaphore_signal(
                barrier, inc=1, device_id={"pairs": position - 1}, device_id_type=MESH
            )

        @pl.when(jnp.logical_not(highest))
        def _():
            pl.semaphore_signal(
                barrier, inc=1, device_id={"pairs": position + 1}, device_id_type=MESH
            )

        greeted = greeted + jnp.where(lowest, 0, 1) + jnp.where(highest, 0, 1)
    pl.semaphore_wait(barrier, greeted)

    if rotates:
        def turn(chunk, carry):
            load(chunk).wait()
            turned = dot_three(split(loaded[at(chunk), :]), (rot_high[...], rot_low[...]), 1)
            left, right = turned[:, :block], turned[:, block:]
            up[at(chunk), :] = jnp.where(lowest, right, left)
            other[at(chunk), :] = jnp.where(lowest, left, right)

            @pl.when(jnp.logical_not(highest))
            def _():
                to_upper(chunk).start()

            @pl.when(highest)
            def _():
                land_second[at(chunk), :] = left

            @pl.when(jnp.logical_not(lowest))
            def _():
                to_lower(chunk).start()

            @pl.when(lowest)
            def _():
                land_first[at(chunk), :] = left

            return carry

        lax.fori_loop(0, CHUNKS, turn, 0)

    if sums:
        cross[...] = jnp.zeros_like(cross)
        norms[...] = jnp.zeros_like(norms)

    def take(chunk, carry):
        if rotates:
            @pl.when(jnp.logical_not(lowest))
            def _():
                to_upper(chunk).wait_recv()

            @pl.when(jnp.logical_not(highest))
            def _():
                to_lower(chunk).wait_recv()

            store(chunk, 0).start()
            store(chunk, 1).start()
        else:
            load(chunk).wait()
        if sums:
            if rotates:
                first, second = land_first[at(chunk), :], land_second[at(chunk), :]
            else:
                first, second = loaded[at(chunk), :block], loaded[at(chunk), block:]
            cross[...] += dot_three(split(first), split(second), 0)
            norms[0:1, :] += jnp.sum(first * first, axis=0, keepdims=True)
            norms[1:2, :] += jnp.sum(second * second, axis=0, keepdims=True)
        return carry

    lax.fori_loop(0, CHUNKS, take, 0)

    if sums:
        share = block // count
        half = block // 2
        for slot in range(count):
            part[slot, :share, :] = cross[slot * share : (slot + 1) * share, :half]
            part[slot, share : 2 * share, :] = cross[slot * share : (slot + 1) * share, half:]
            part[slot, 2 * share : 2 * share + 8, :] = norms[:, :half]
            part[slot, 2 * share + 8 : 2 * share + 16, :] = norms[:, half:]
        sum_over_rows(count, part, total, recv, mine, gathered, sums_sems)

    if rotates:
        def finish(chunk, carry):
            @pl.when(jnp.logical_not(highest))
            def _():
                to_upper(chunk).wait_send()

            @pl.when(jnp.logical_not(lowest))
            def _():
                to_lower(chunk).wait_send()

            store(chunk, 0).wait()
            store(chunk, 1).wait()
            return carry

        lax.fori_loop(0, CHUNKS, finish, 0)


def stage(name, number, matrix, rotation, sums):
    rows, cols = matrix.shape
    block = cols // 2
    count = lax.axis_size("rows")
    length = lax.axis_size("pairs")
    rotates = rotation is not None
    slot = (2 * (block // count) + 16, block // 2)
    hbm = pl.BlockSpec(memory_space=pl.ANY)
    vmem = pl.BlockSpec(memory_space=pltpu.VMEM)
    dma = pltpu.SemaphoreType.DMA
    in_specs, outs, out_specs = [hbm], [], []
    scratch = [pltpu.VMEM((rows, cols), F32), dma((CHUNKS,))]
    if rotates:
        in_specs += [vmem, vmem]
        outs.append(jax.ShapeDtypeStruct((rows, cols), F32))
        out_specs.append(hbm)
        scratch += [pltpu.VMEM((rows, block), F32)] * 4
        scratch += [dma((CHUNKS,))] * 4 + [dma((2, CHUNKS))]
    if sums:
        outs.append(jax.ShapeDtypeStruct((count,) + slot, F32))
        out_specs.append(vmem)
        scratch += [pltpu.VMEM((block, block), F32), pltpu.VMEM((8, block), F32)]
        scratch += [pltpu.VMEM((count,) + slot, F32)] * 2 + [pltpu.VMEM(slot, F32)]
        scratch += [pltpu.VMEM((count,) + slot, F32)]
        scratch += [dma((count,))] * 4
    return pl.pallas_call(
        functools.partial(stage_kernel, rotates, sums, count, length),
        out_shape=outs,
        in_specs=in_specs,
        out_specs=out_specs,
        scratch_shapes=scratch,
        name=name,
        compiler_params=pltpu.CompilerParams(
            collective_id=number, has_side_effects=True, vmem_limit_bytes=50 * 2**20
        ),
    )(matrix, *(rotation or ()))


def rotation_kernel(rows_all, total, rot_high, rot_low, coupling, inverse, residual):
    count, depth, half = total.shape
    block = 2 * half
    share = (depth - 16) // 2
    for slot in range(count):
        coupling[slot * share : (slot + 1) * share, :half] = total[slot, :share, :]
        coupling[slot * share : (slot + 1) * share, half:] = total[slot, share : 2 * share, :]
    norms = jnp.concatenate(
        [total[0, 2 * share : 2 * share + 8, :], total[0, 2 * share + 8 :, :]], axis=1
    )
    scales = lax.rsqrt(norms / rows_all + 1e-06)
    row = lax.broadcasted_iota(jnp.int32, (block, block), 0)
    col = lax.broadcasted_iota(jnp.int32, (block, block), 1)
    identity = jnp.where(row == col, 1.0, 0.0).astype(F32)
    scale_first = jnp.sum(identity * scales[0:1, :], axis=1, keepdims=True)
    coupling[...] = 0.5 * coupling[...] * scale_first * scales[1:2, :] / rows_all
    turn = coupling[...]
    gram = lax.dot_general(
        turn,
        turn,
        (((1,), (1,)), ((), ())),
        precision=lax.Precision.HIGHEST,
        preferred_element_type=F32,
    )
    spread = jnp.max(jnp.sum(jnp.abs(gram), axis=1, keepdims=True))
    start = 2.0 / (2.0 + spread)
    first = (1.0 - start) * identity - start * gram
    inverse[...] = start * (identity + first)
    bound = spread / (2.0 + spread)
    residual[...] = exact_dot(first, first)

    def grow(state):
        limit, trips = state
        both = exact_dot(jnp.concatenate([inverse[...], residual[...]], axis=0), residual[...])
        inverse[...] += both[:block]
        residual[...] = both[block:]
        return limit * limit, trips + 1

    lax.while_loop(
        lambda state: jnp.logical_and(state[0] > 1e-07, state[1] < 30),
        grow,
        (bound * bound, jnp.int32(0)),
    )

    def correct(index, carry):
        guess = inverse[...]
        residual[...] = identity - guess - exact_dot(gram, guess)
        inverse[...] = guess + exact_dot(guess, residual[...])
        return carry

    lax.fori_loop(0, jnp.where(spread > 32.0, 4, 0), correct, 0)
    upper = exact_dot(inverse[...], turn)
    lower = exact_dot(turn, upper, 0)
    parts = (
        (0, 0, 2.0 * inverse[...] - identity),
        (0, 1, 2.0 * upper),
        (1, 0, -2.0 * upper.T),
        (1, 1, identity - 2.0 * lower),
    )
    for down, across, value in parts:
        high, low = split(value)
        where = (pl.ds(down * block, block), pl.ds(across * block, block))
        rot_high[where] = high
        rot_low[where] = low


def rotation_of(total, rows_all):
    block = 2 * total.shape[2]
    vmem = pl.BlockSpec(memory_space=pltpu.VMEM)
    return pl.pallas_call(
        functools.partial(rotation_kernel, rows_all),
        out_shape=[jax.ShapeDtypeStruct((2 * block, 2 * block), BF16)] * 2,
        in_specs=[vmem],
        out_specs=[vmem, vmem],
        scratch_shapes=[pltpu.VMEM((block, block), F32)] * 3,
        name="rotation",
        compiler_params=pltpu.CompilerParams(vmem_limit_bytes=32 * 2**20),
    )(total)


def shards(matrix):
    rows_all = matrix.shape[0] * lax.axis_size("rows")
    (total,) = stage("products", 0, matrix, None, True)
    for turn_index in range(STEPS - 1):
        rotation = rotation_of(total, rows_all)
        matrix, total = stage("turn_and_products", 1, matrix, rotation, True)
    rotation = rotation_of(total, rows_all)
    (matrix,) = stage("last_turn", 2, matrix, rotation, False)
    return matrix


def solution(mesh):
    return jax.shard_map(
        shards,
        mesh=mesh,
        in_specs=(P("rows", "pairs"),),
        out_specs=P("rows", "pairs"),
        check_vma=False,
    )
```

profile of v0, /device:TPU:1, one launch (start us, length us, event | category | flops | bytes accessed | tf_op | source)
XLA Modules:
  0.0 108.6 jit_solution(3396030664486308395)
XLA Ops:
  0.0 20.1 %products.1.total = f32[8,80,128]{2,1,0:T(8,128)S(1)} custom-call(f32[2048,512]{1,0:T(8,128)} %refs_0_.3), custom_call_target="tpu_custom_call" | custom-call | tf_op jit(solution)/shard_map/products/pallas_call | solution.py:286
  20.1 5.5 %rotation.2 = (bf16[512,512]{1,0:T(8,128)(2,1)S(1)}, bf16[512,512]{1,0:T(8,128)(2,1)S(1)}) custom-call(f32[8,80,128]{2,1,0:T(8,128)S(1)} %products.1.total), custom_call_target="tpu_custom_call" | custom-call | tf_op jit(solution)/shard_map/rotation/pallas_call | solution.py:368
  25.6 44.6 %turn_and_products.1 = (f32[2048,512]{1,0:T(8,128)}, f32[8,80,128]{2,1,0:T(8,128)S(1)}) custom-call(f32[2048,512]{1,0:T(8,128)} %refs_0_.3, bf16[512,512]{1,0:T(8,128)(2,1)S(1)} %get-tuple-element.11.refs_1_, bf16[512,512]{1,0:T(8,128)(2,1)S(1)} %get-tuple-element.12.refs_2_), custom_call_target="tpu_custom_call" | custom-call | tf_op jit(solution)/shard_map/turn_and_products/pallas_call | solution.py:286
  70.2 5.5 %rotation.3 = (bf16[512,512]{1,0:T(8,128)(2,1)S(1)}, bf16[512,512]{1,0:T(8,128)(2,1)S(1)}) custom-call(f32[8,80,128]{2,1,0:T(8,128)S(1)} %get-tuple-element.14.total), custom_call_target="tpu_custom_call" | custom-call | tf_op jit(solution)/shard_map/rotation/pallas_call | solution.py:368
  75.8 28.2 %last_turn.1 = f32[2048,512]{1,0:T(8,128)} custom-call(f32[2048,512]{1,0:T(8,128)} %get-tuple-element.13.refs_0_, bf16[512,512]{1,0:T(8,128)(2,1)S(1)} %get-tuple-element.15.refs_1_, bf16[512,512]{1,0:T(8,128)(2,1)S(1)} %get-tuple-element.16.refs_2_), custom_call_target="tpu_custom_call" | custom-call | tf_op jit(solution)/shard_map/last_turn/pallas_call | solution.py:286
  104.0 4.6 %copy.3 = f32[2048,512]{1,0:T(8,128)} copy(f32[2048,512]{1,0:T(8,128)} %last_turn.1) | data formatting | bytes 8388608
where the time goes:
time: 109 us
  Pallas kernels  104 us (95%)
  local copies, waits for them, and re-layouts  4.64 us (4%)
    pallas_call x3, Pallas kernels, stage(): pl.pallas_call(functools.partial(stage_kernel, rotates, sums, count, leng...  92.9 us
    pallas_call x2, Pallas kernels, rotation_of(): pl.pallas_call(functools.partial(rotation_kernel, rows_all), out_shape=[j...  11 us
    unnamed x1, local copies, waits for them, and re-layouts  4.64 us

commit v1 on v0

v1 whole, which is shorter than its diff:
```python
import functools

import jax
import jax.numpy as jnp
from jax import lax
from jax.experimental import pallas as pl
from jax.experimental.pallas import tpu as pltpu
from jax.sharding import PartitionSpec as P

CHUNKS = 8
EARLY = 4
F32 = jnp.float32
BF16 = jnp.bfloat16
MESH = pl.DeviceIdType.MESH
DMA = pltpu.SemaphoreType.DMA


def split(value):
    high = value.astype(BF16)
    return high, (value - high.astype(F32)).astype(BF16)


def dot_bf16(left, right, left_dim):
    return lax.dot_general(
        left, right, (((left_dim,), (0,)), ((), ())), preferred_element_type=F32
    )


def dot_three(left, right, left_dim):
    return (
        dot_bf16(left[0], right[1], left_dim)
        + dot_bf16(left[1], right[0], left_dim)
        + dot_bf16(left[0], right[0], left_dim)
    )


def exact_dot(left, right, left_dim=1, right_dim=0):
    return lax.dot_general(
        left,
        right,
        (((left_dim,), (right_dim,)), ((), ())),
        precision=lax.Precision.HIGHEST,
        preferred_element_type=F32,
    )


def rows_copy(src, dst, send, recv, peer):
    return pltpu.make_async_remote_copy(
        src_ref=src,
        dst_ref=dst,
        send_sem=send,
        recv_sem=recv,
        device_id={"rows": peer},
        device_id_type=MESH,
    )


def pairs_copy(src, dst, send, recv, peer):
    return pltpu.make_async_remote_copy(
        src_ref=src,
        dst_ref=dst,
        send_sem=send,
        recv_sem=recv,
        device_id={"pairs": peer},
        device_id_type=MESH,
    )


def greet(barrier, axis, peer):
    pl.semaphore_signal(barrier, inc=1, device_id={axis: peer}, device_id_type=MESH)


def partners(position, length):
    even = position % 2 == 0
    down = jnp.where(position == 0, 1, position - 2)
    up = jnp.where(position == length - 1, length - 2, position + 2)
    lead = jnp.where(even, down, up)
    down = jnp.where(position == 1, 0, position - 2)
    up = jnp.where(position == length - 2, length - 1, position + 2)
    keep = jnp.where(even, up, down)
    return lead, keep


def pack(count, cross, norms, part):
    block = cross.shape[0]
    share = block // count
    half = block // 2
    for slot in range(count):
        part[slot, :share, :] = cross[slot * share : (slot + 1) * share, :half]
        part[slot, share : 2 * share, :] = cross[slot * share : (slot + 1) * share, half:]
        part[slot, 2 * share : 2 * share + 8, :] = norms[:, :half]
        part[slot, 2 * share + 8 : 2 * share + 16, :] = norms[:, half:]


def unpack(total, cross):
    count, depth, half = total.shape
    share = (depth - 16) // 2
    for slot in range(count):
        cross[slot * share : (slot + 1) * share, :half] = total[slot, :share, :]
        cross[slot * share : (slot + 1) * share, half:] = total[slot, share : 2 * share, :]
    return jnp.concatenate(
        [total[0, 2 * share : 2 * share + 8, :], total[0, 2 * share + 8 :, :]], axis=1
    )


def scatter_sum(count, part, recv, mine, send_sems, recv_sems):
    me = lax.axis_index("rows")
    copies = []
    for far in range(1, count):
        peer = lax.rem(me + far, count)
        copy = rows_copy(part.at[peer], recv.at[far], send_sems.at[far], recv_sems.at[far], peer)
        copy.start()
        copies.append(copy)
    acc = part[me]
    for far in range(1, count):
        copies[far - 1].wait_recv()
        acc = acc + recv[far]
    mine[...] = acc
    return copies


def gather_start(count, mine, gathered, send_sems, recv_sems):
    me = lax.axis_index("rows")
    copies = []
    for far in range(1, count):
        peer = lax.rem(me + far, count)
        copy = rows_copy(mine, gathered.at[far], send_sems.at[far], recv_sems.at[far], peer)
        copy.start()
        copies.append(copy)
    return copies


def gather_finish(count, mine, gathered, total, copies):
    me = lax.axis_index("rows")
    total[me] = mine[...]
    for far in range(1, count):
        copies[far - 1].wait_recv()
        total[lax.rem(me + count - far, count)] = gathered[far]


def products_kernel(count, matrix, total, loaded, load_sem, cross, norms, part, recv, mine, gathered, *sems):
    rows, cols = loaded.shape
    block = cols // 2
    step = rows // CHUNKS

    def at(chunk):
        return pl.ds(pl.multiple_of(chunk * step, step), step)

    def load(chunk):
        return pltpu.make_async_copy(
            matrix.at[at(chunk)], loaded.at[at(chunk)], load_sem.at[chunk]
        )

    for chunk in range(CHUNKS):
        load(chunk).start()
    barrier = pltpu.get_barrier_semaphore()
    me = lax.axis_index("rows")
    for far in range(1, count):
        greet(barrier, "rows", lax.rem(me + far, count))
    cross[...] = jnp.zeros_like(cross)
    norms[...] = jnp.zeros_like(norms)

    def take(chunk, carry):
        load(chunk).wait()
        first, second = loaded[at(chunk), :block], loaded[at(chunk), block:]
        cross[...] += dot_three(split(first), split(second), 0)
        norms[0:1, :] += jnp.sum(first * first, axis=0, keepdims=True)
        norms[1:2, :] += jnp.sum(second * second, axis=0, keepdims=True)
        return carry

    lax.fori_loop(0, CHUNKS, take, 0)
    pack(count, cross, norms, part)
    pl.semaphore_wait(barrier, count - 1)
    copies = scatter_sum(count, part, recv, mine, sems[0], sems[1])
    more = gather_start(count, mine, gathered, sems[2], sems[3])
    gather_finish(count, mine, gathered, total, more)
    for copy in copies + more:
        copy.wait_send()


def products(matrix):
    rows, cols = matrix.shape
    block = cols // 2
    count = lax.axis_size("rows")
    slot = (2 * (block // count) + 16, block // 2)
    return pl.pallas_call(
        functools.partial(products_kernel, count),
        out_shape=jax.ShapeDtypeStruct((count,) + slot, F32),
        in_specs=[pl.BlockSpec(memory_space=pl.ANY)],
        out_specs=pl.BlockSpec(memory_space=pltpu.VMEM),
        scratch_shapes=[
            pltpu.VMEM((rows, cols), F32),
            DMA((CHUNKS,)),
            pltpu.VMEM((block, block), F32),
            pltpu.VMEM((8, block), F32),
            pltpu.VMEM((count,) + slot, F32),
            pltpu.VMEM((count,) + slot, F32),
            pltpu.VMEM(slot, F32),
            pltpu.VMEM((count,) + slot, F32),
        ]
        + [DMA((count,))] * 4,
        name="products",
        compiler_params=pltpu.CompilerParams(
            collective_id=0, has_side_effects=True, vmem_limit_bytes=24 * 2**20
        ),
    )(matrix)


def exchange_kernel(
    count, length, matrix, rot_high, rot_low,
    lead, keep, lead_land, keep_land, total_keep, total_lead,
    loaded, cross, norms, part, recv, mine, gathered, passed, gathered_lead,
    load_sem, lead_send, lead_recv, keep_send, keep_recv,
    sum_send, sum_recv, all_send, all_recv, pass_send, pass_recv, more_send, more_recv, go_sem,
):
    rows, cols = loaded.shape
    block = cols // 2
    step = rows // CHUNKS
    me = lax.axis_index("rows")
    position = lax.axis_index("pairs")
    lead_peer, keep_peer = partners(position, length)
    core_peer = position + 1 - 2 * (position % 2)
    near = keep_peer == core_peer
    left_leads = jnp.logical_or(position % 2 == 1, position == 0)
    signals = jnp.logical_and(position > 0, position < length - 1)

    def at(chunk):
        return pl.ds(pl.multiple_of(chunk * step, step), step)

    def load(chunk):
        return pltpu.make_async_copy(
            matrix.at[at(chunk)], loaded.at[at(chunk)], load_sem.at[chunk]
        )

    def send_lead(chunk):
        return pairs_copy(
            lead.at[at(chunk)], keep_land.at[at(chunk)],
            lead_send.at[chunk], lead_recv.at[chunk], lead_peer,
        )

    def send_keep(chunk):
        return pairs_copy(
            keep.at[at(chunk)], lead_land.at[at(chunk)],
            keep_send.at[chunk], keep_recv.at[chunk], keep_peer,
        )

    def loop(low, high, do):
        def body(chunk, carry):
            do(chunk)
            return carry

        lax.fori_loop(low, high, body, 0)

    for chunk in range(CHUNKS):
        load(chunk).start()
    barrier = pltpu.get_barrier_semaphore()
    for far in range(1, count):
        greet(barrier, "rows", lax.rem(me + far, count))
    for peer in (lead_peer, keep_peer, core_peer):
        greet(barrier, "pairs", peer)
    pl.semaphore_wait(barrier, count + 2)

    def turn(chunk):
        load(chunk).wait()
        turned = dot_three(split(loaded[at(chunk), :]), (rot_high[...], rot_low[...]), 1)
        left, right = turned[:, :block], turned[:, block:]
        lead[at(chunk), :] = jnp.where(left_leads, left, right)
        keep[at(chunk), :] = jnp.where(left_leads, right, left)
        send_lead(chunk).start()

        @pl.when(near)
        def _():
            send_keep(chunk).start()

    loop(0, CHUNKS, turn)
    cross[...] = jnp.zeros_like(cross)
    norms[...] = jnp.zeros_like(norms)

    def take(chunk):
        send_lead(chunk).wait_recv()
        mine_rows, theirs = keep[at(chunk), :], keep_land[at(chunk), :]
        cross[...] += dot_three(split(mine_rows), split(theirs), 0)
        norms[0:1, :] += jnp.sum(mine_rows * mine_rows, axis=0, keepdims=True)
        norms[1:2, :] += jnp.sum(theirs * theirs, axis=0, keepdims=True)

    def hand_over():
        loop(0, CHUNKS - 1, lambda chunk: send_lead(chunk).wait_send())

        @pl.when(signals)
        def _():
            pl.semaphore_signal(
                go_sem, inc=1, device_id={"pairs": core_peer}, device_id_type=MESH
            )

    loop(0, CHUNKS - 1, take)

    @pl.when(jnp.logical_not(near))
    def _():
        hand_over()
        pl.semaphore_wait(go_sem, 1)
        loop(0, EARLY, lambda chunk: send_keep(chunk).start())

    take(CHUNKS - 1)
    pack(count, cross, norms, part)
    copies = scatter_sum(count, part, recv, mine, sum_send, sum_recv)
    piece = pairs_copy(mine, passed, pass_send, pass_recv, keep_peer)
    piece.start()
    more = gather_start(count, mine, gathered, all_send, all_recv)

    @pl.when(jnp.logical_not(near))
    def _():
        loop(EARLY, CHUNKS, lambda chunk: send_keep(chunk).start())

    gather_finish(count, mine, gathered, total_keep, more)

    @pl.when(near)
    def _():
        hand_over()

    piece.wait_recv()
    rest = gather_start(count, passed, gathered_lead, more_send, more_recv)
    gather_finish(count, passed, gathered_lead, total_lead, rest)
    for copy in copies + more + rest + [piece]:
        copy.wait_send()
    send_lead(CHUNKS - 1).wait_send()
    loop(0, CHUNKS, lambda chunk: send_keep(chunk).wait())


def exchange(matrix, rotation, slot):
    rows, cols = matrix.shape
    block = cols // 2
    count = lax.axis_size("rows")
    length = lax.axis_size("pairs")
    vmem = pl.BlockSpec(memory_space=pltpu.VMEM)
    pieces = (count,) + slot
    return pl.pallas_call(
        functools.partial(exchange_kernel, count, length),
        out_shape=[jax.ShapeDtypeStruct((rows, block), F32)] * 4
        + [jax.ShapeDtypeStruct(pieces, F32)] * 2,
        in_specs=[pl.BlockSpec(memory_space=pl.ANY), vmem, vmem],
        out_specs=[vmem] * 6,
        scratch_shapes=[
            pltpu.VMEM((rows, cols), F32),
            pltpu.VMEM((block, block), F32),
            pltpu.VMEM((8, block), F32),
            pltpu.VMEM(pieces, F32),
            pltpu.VMEM(pieces, F32),
            pltpu.VMEM(slot, F32),
            pltpu.VMEM(pieces, F32),
            pltpu.VMEM(slot, F32),
            pltpu.VMEM(pieces, F32),
        ]
        + [DMA((CHUNKS,))] * 5
        + [DMA((count,))] * 4
        + [DMA(()), DMA(())]
        + [DMA((count,))] * 2
        + [pltpu.SemaphoreType.REGULAR],
        name="exchange",
        compiler_params=pltpu.CompilerParams(
            collective_id=1, has_side_effects=True, vmem_limit_bytes=32 * 2**20
        ),
    )(matrix, *rotation)


def identity_of(block):
    row = lax.broadcasted_iota(jnp.int32, (block, block), 0)
    col = lax.broadcasted_iota(jnp.int32, (block, block), 1)
    return jnp.where(row == col, 1.0, 0.0).astype(F32)


def couple(rows_all, norms, cross, identity):
    scales = lax.rsqrt(norms / rows_all + 1e-06)
    scale_first = jnp.sum(identity * scales[0:1, :], axis=1, keepdims=True)
    cross[...] = 0.5 * cross[...] * scale_first * scales[1:2, :] / rows_all


def invert(grams, inverses, residuals, identity):
    block = identity.shape[0]
    spreads = [jnp.max(jnp.sum(jnp.abs(gram), axis=1, keepdims=True)) for gram in grams]
    for gram, spread, inverse, residual in zip(grams, spreads, inverses, residuals):
        start = 2.0 / (2.0 + spread)
        first = (1.0 - start) * identity - start * gram
        inverse[...] = start * (identity + first)
        residual[...] = exact_dot(first, first)
    spread = functools.reduce(jnp.maximum, spreads)
    bound = spread / (2.0 + spread)

    def grow(state):
        limit, trips = state
        for inverse, residual in zip(inverses, residuals):
            both = exact_dot(jnp.concatenate([inverse[...], residual[...]], axis=0), residual[...])
            inverse[...] += both[:block]
            residual[...] = both[block:]
        return limit * limit, trips + 1

    lax.while_loop(
        lambda state: jnp.logical_and(state[0] > 1e-07, state[1] < 30),
        grow,
        (bound * bound, jnp.int32(0)),
    )

    def correct(index, carry):
        for gram, inverse, residual in zip(grams, inverses, residuals):
            guess = inverse[...]
            residual[...] = identity - guess - exact_dot(gram, guess)
            inverse[...] = guess + exact_dot(guess, residual[...])
        return carry

    lax.fori_loop(0, jnp.where(spread > 32.0, 4, 0), correct, 0)


def rotation_kernel(rows_all, total, rot_high, rot_low, coupling, inverse, residual):
    block = coupling.shape[0]
    norms = unpack(total, coupling)
    identity = identity_of(block)
    couple(rows_all, norms, coupling, identity)
    turn = coupling[...]
    gram = exact_dot(turn, turn, 1, 1)
    invert([gram], [inverse], [residual], identity)
    upper = exact_dot(inverse[...], turn)
    lower = exact_dot(turn, upper, 0)
    parts = (
        (0, 0, 2.0 * inverse[...] - identity),
        (0, 1, 2.0 * upper),
        (1, 0, -2.0 * upper.T),
        (1, 1, identity - 2.0 * lower),
    )
    for down, across, value in parts:
        high, low = split(value)
        where = (pl.ds(down * block, block), pl.ds(across * block, block))
        rot_high[where] = high
        rot_low[where] = low


def rotation_of(total, rows_all):
    block = 2 * total.shape[2]
    vmem = pl.BlockSpec(memory_space=pltpu.VMEM)
    return pl.pallas_call(
        functools.partial(rotation_kernel, rows_all),
        out_shape=[jax.ShapeDtypeStruct((2 * block, 2 * block), BF16)] * 2,
        in_specs=[vmem],
        out_specs=[vmem, vmem],
        scratch_shapes=[pltpu.VMEM((block, block), F32)] * 3,
        name="rotation",
        compiler_params=pltpu.CompilerParams(vmem_limit_bytes=16 * 2**20),
    )(total)


def final_kernel(
    rows_all, place, lead, keep, lead_land, keep_land, total_keep, total_lead, out,
    turns, inverses, residuals, high, low, staged, sems,
):
    rows, block = lead.shape
    step = rows // CHUNKS
    position, length = place[0], place[1]
    identity = identity_of(block)
    couplings = [turns.at[0], turns.at[1]]
    own_out = [position == 1, position == 0]
    flips = [jnp.logical_not(own_out[0]), own_out[1]]
    odd = position % 2 == 1
    grams = []
    for index, total in enumerate((total_keep, total_lead)):
        norms = unpack(total, couplings[index])
        couple(rows_all, norms, couplings[index], identity)
        value = couplings[index][...]
        couplings[index][...] = jnp.where(flips[index], value.T, value)
        value = couplings[index][...]
        grams.append(exact_dot(value, value, 1, 1))
    invert(
        grams,
        [inverses.at[0], inverses.at[1]],
        [residuals.at[0], residuals.at[1]],
        identity,
    )
    first_slot = [odd, jnp.logical_not(odd)]
    for index in range(2):
        takes_first = jnp.where(
            first_slot[index], position != 1, position == length - 1
        )
        inverse = inverses[index]
        straight = 2.0 * inverse - identity
        sign = jnp.where(takes_first, -2.0, 2.0)
        crossed = sign * exact_dot(couplings[index][...], inverse, 0)
        own = jnp.where(own_out[index], straight, crossed)
        landed = jnp.where(own_out[index], crossed, straight)
        for part, value in enumerate((own, landed)):
            top, bottom = split(value)
            high[index, part] = top
            low[index, part] = bottom

    def at(chunk):
        return pl.ds(pl.multiple_of(chunk * step, step), step)

    def store(chunk, index):
        column = jnp.where(first_slot[index], 0, block)
        return pltpu.make_async_copy(
            staged.at[index, at(chunk)],
            out.at[at(chunk), pl.ds(pl.multiple_of(column, block), block)],
            sems.at[index, chunk],
        )

    def body(chunk, carry):
        for index, (own, landed) in enumerate(((keep, keep_land), (lead, lead_land))):
            staged[index, at(chunk), :] = dot_three(
                split(own[at(chunk), :]), (high[index, 0], low[index, 0]), 1
            ) + dot_three(split(landed[at(chunk), :]), (high[index, 1], low[index, 1]), 1)
            store(chunk, index).start()
        return carry

    lax.fori_loop(0, CHUNKS, body, 0)

    def drain(chunk, carry):
        store(chunk, 0).wait()
        store(chunk, 1).wait()
        return carry

    lax.fori_loop(0, CHUNKS, drain, 0)


def final(rows_all, blocks, totals):
    rows, block = blocks[0].shape
    vmem = pl.BlockSpec(memory_space=pltpu.VMEM)
    place = jnp.stack([lax.axis_index("pairs"), jnp.int32(lax.axis_size("pairs"))])
    return pl.pallas_call(
        functools.partial(final_kernel, rows_all),
        out_shape=jax.ShapeDtypeStruct((rows, 2 * block), F32),
        in_specs=[pl.BlockSpec(memory_space=pltpu.SMEM)] + [vmem] * 6,
        out_specs=pl.BlockSpec(memory_space=pl.ANY),
        scratch_shapes=[
            pltpu.VMEM((2, block, block), F32),
            pltpu.VMEM((2, block, block), F32),
            pltpu.VMEM((2, block, block), F32),
            pltpu.VMEM((2, 2, block, block), BF16),
            pltpu.VMEM((2, 2, block, block), BF16),
            pltpu.VMEM((2, rows, block), F32),
            DMA((2, CHUNKS)),
        ],
        name="final",
        compiler_params=pltpu.CompilerParams(vmem_limit_bytes=32 * 2**20),
    )(place, *blocks, *totals)


def shards(matrix):
    rows_all = matrix.shape[0] * lax.axis_size("rows")
    total = products(matrix)
    rotation = rotation_of(total, rows_all)
    moved = exchange(matrix, rotation, total.shape[1:])
    return final(rows_all, moved[:4], moved[4:])


def solution(mesh):
    return jax.shard_map(
        shards,
        mesh=mesh,
        in_specs=(P("rows", "pairs"),),
        out_specs=P("rows", "pairs"),
        check_vma=False,
    )
```

time: 109 us -> 97.4 us (0.89)
  Pallas kernels: 104 us -> 94.2 us
  local copies, waits for them, and re-layouts: 4.64 us -> 2.19 us
    pallas_call x2 -> x1, Pallas kernels: 11 us -> 5.52 us  [rotation_of(): pl.pallas_call(functools.partial(rotation_kernel, rows_all), out_shape=[j...]
    pallas_call x3, Pallas kernels: 92.9 us -> 88.7 us  [the longest x1 56.8 us: exchange(): pl.pallas_call(functools.partial(exchange_kernel, count, length), out_sha...]
    unnamed x1 -> x4, local copies, waits for them, and re-layouts: 4.64 us -> 2.19 us
where the time goes in v1:
time: 97.4 us; the launch traced here: 96.5 us
  Pallas kernels  94.2 us (97%)
  local copies, waits for them, and re-layouts  2.19 us (2%)
    pallas_call x1, Pallas kernels, exchange(): pl.pallas_call(functools.partial(exchange_kernel, count, length), out_sha...  56.8 us
    pallas_call x1, Pallas kernels, products(): pl.pallas_call(functools.partial(products_kernel, count), out_shape=jax.S...  17.7 us
    pallas_call x1, Pallas kernels, final(): pl.pallas_call(functools.partial(final_kernel, rows_all), out_shape=jax.S...  14.2 us
    pallas_call x1, Pallas kernels, rotation_of(): pl.pallas_call(functools.partial(rotation_kernel, rows_all), out_shape=[j...  5.52 us
    unnamed x4, local copies, waits for them, and re-layouts  2.19 us

profile of v1, /device:TPU:1, one launch (start us, length us, event | category | flops | bytes accessed | tf_op | source)
XLA Modules:
  0.0 96.5 jit_solution(11772043367932427791)
XLA Ops:
  0.0 0.1 pad_add_fusion.place
  0.1 0.0 copy-start
  0.1 2.2 %copy-done = f32[2048,512]{1,0:T(8,128)S(1)} copy-done((f32[2048,512]{1,0:T(8,128)S(1)}, f32[2048,512]{1,0:T(8,128)}, u32[]{:S(2)}) %copy-start) | copy-done | bytes 4194328
  2.3 0.0 copy-start.1
  2.3 17.7 %products.1.total = f32[8,80,128]{2,1,0:T(8,128)S(1)} custom-call(f32[2048,512]{1,0:T(8,128)S(1)} %copy-done), custom_call_target="tpu_custom_call" | custom-call | tf_op jit(solution)/shard_map/products/pallas_call | solution.py:186
  20.0 5.5 %rotation.1 = (bf16[512,512]{1,0:T(8,128)(2,1)S(1)}, bf16[512,512]{1,0:T(8,128)(2,1)S(1)}) custom-call(f32[8,80,128]{2,1,0:T(8,128)S(1)} %products.1.total), custom_call_target="tpu_custom_call" | custom-call | tf_op jit(solution)/shard_map/rotation/pallas_call | solution.py:438
  25.5 0.0 copy-done.1
  25.5 56.8 %exchange.1 = (f32[2048,256]{1,0:T(8,128)S(1)}, f32[2048,256]{1,0:T(8,128)S(1)}, f32[2048,256]{1,0:T(8,128)S(1)}, f32[2048,256]{1,0:T(8,128)S(1)}, f32[8,80,128]{2,1,0:T(8,128)S(1)}, /*index=5*/f32[8,80,128]{2,1,0:T(8,128)S(1)}) custom-call(f32[2048,512]{1,0:T(8,128)S(1)} %copy-done.1, bf16[512,512]{1,0:T(8,128)(2,1)S(1)} %get-tuple-element.13.rot_high, ...), custom_call_target="tpu_custom_call" | custom-call | tf_op jit(solution)/shard_map/exchange/pallas_call | solution.py:336
  82.3 14.2 %final.1 = f32[2048,512]{1,0:T(8,128)} custom-call(s32[2]{0:T(128)S(1)} %pad_add_fusion.place, f32[2048,256]{1,0:T(8,128)S(1)} %get-tuple-element.15.lead, f32[2048,256]{1,0:T(8,128)S(1)} %get-tuple-element.16.keep, f32[2048,256]{1,0:T(8,128)S(1)} %get-tuple-element.17.lead_land, f32[2048,256]{1,0:T(8,128)S(1)} %get-tuple-element.18.keep_land, ...), custom_call_target="tpu_custom_call" | custom-call | tf_op jit(solution)/shard_map/final/pallas_call | solution.py:524
Async XLA Ops:
  0.1 2.2 %copy-start = (f32[2048,512]{1,0:T(8,128)S(1)}, f32[2048,512]{1,0:T(8,128)}, u32[]{:S(2)}) copy-start(f32[2048,512]{1,0:T(8,128)} %matrix.3) | copy-start | bytes 12582916
  2.3 23.2 %copy-start.1 = (f32[2048,512]{1,0:T(8,128)S(1)}, f32[2048,512]{1,0:T(8,128)}, u32[]{:S(2)}) copy-start(f32[2048,512]{1,0:T(8,128)} %matrix.3) | copy-start | bytes 12582916

commit v2 on v1

--- a/solution.py
+++ b/solution.py
@@ -9,6 +9,7 @@
 
 CHUNKS = 8
 EARLY = 4
+STORES = 4
 F32 = jnp.float32
 BF16 = jnp.bfloat16
 MESH = pl.DeviceIdType.MESH
@@ -81,6 +82,14 @@
     return lead, keep
 
 
+def add_norms(norms, first, second):
+    half = norms.shape[1]
+    for row, value in ((0, first), (1, second)):
+        sums = jnp.sum(value * value, axis=0, keepdims=True)
+        norms[row : row + 1, :] += sums[:, :half]
+        norms[row + 4 : row + 5, :] += sums[:, half:]
+
+
 def pack(count, cross, norms, part):
     block = cross.shape[0]
     share = block // count
@@ -88,19 +97,17 @@
     for slot in range(count):
         part[slot, :share, :] = cross[slot * share : (slot + 1) * share, :half]
         part[slot, share : 2 * share, :] = cross[slot * share : (slot + 1) * share, half:]
-        part[slot, 2 * share : 2 * share + 8, :] = norms[:, :half]
-        part[slot, 2 * share + 8 : 2 * share + 16, :] = norms[:, half:]
+        part[slot, 2 * share : 2 * share + 8, :] = norms[...]
 
 
 def unpack(total, cross):
     count, depth, half = total.shape
-    share = (depth - 16) // 2
+    share = (depth - 8) // 2
     for slot in range(count):
         cross[slot * share : (slot + 1) * share, :half] = total[slot, :share, :]
         cross[slot * share : (slot + 1) * share, half:] = total[slot, share : 2 * share, :]
-    return jnp.concatenate(
-        [total[0, 2 * share : 2 * share + 8, :], total[0, 2 * share + 8 :, :]], axis=1
-    )
+    norms = total[0, 2 * share :, :]
+    return jnp.concatenate([norms[0:4], norms[4:8]], axis=1)
 
 
 def scatter_sum(count, part, recv, mine, send_sems, recv_sems):
@@ -164,8 +171,7 @@
         load(chunk).wait()
         first, second = loaded[at(chunk), :block], loaded[at(chunk), block:]
         cross[...] += dot_three(split(first), split(second), 0)
-        norms[0:1, :] += jnp.sum(first * first, axis=0, keepdims=True)
-        norms[1:2, :] += jnp.sum(second * second, axis=0, keepdims=True)
+        add_norms(norms, first, second)
         return carry
 
     lax.fori_loop(0, CHUNKS, take, 0)
@@ -182,17 +188,19 @@
     rows, cols = matrix.shape
     block = cols // 2
     count = lax.axis_size("rows")
-    slot = (2 * (block // count) + 16, block // 2)
+    slot = (2 * (block // count) + 8, block // 2)
     return pl.pallas_call(
         functools.partial(products_kernel, count),
-        out_shape=jax.ShapeDtypeStruct((count,) + slot, F32),
-        in_specs=[pl.BlockSpec(memory_space=pl.ANY)],
-        out_specs=pl.BlockSpec(memory_space=pltpu.VMEM),
+        out_shape=[
+            jax.ShapeDtypeStruct((count,) + slot, F32),
+            jax.ShapeDtypeStruct((rows, cols), F32),
+        ],
+        in_specs=[pl.BlockSpec(memory_space=pltpu.HBM)],
+        out_specs=[pl.BlockSpec(memory_space=pltpu.VMEM)] * 2,
         scratch_shapes=[
-            pltpu.VMEM((rows, cols), F32),
             DMA((CHUNKS,)),
             pltpu.VMEM((block, block), F32),
-            pltpu.VMEM((8, block), F32),
+            pltpu.VMEM((8, block // 2), F32),
             pltpu.VMEM((count,) + slot, F32),
             pltpu.VMEM((count,) + slot, F32),
             pltpu.VMEM(slot, F32),
@@ -206,14 +214,46 @@
     )(matrix)
 
 
+def invert_fixed(gram, inverse, residual, identity):
+    block = identity.shape[0]
+    largest = 0.25 * block * block
+    ratio, trips = largest / (2.0 + largest), 0
+    while ratio > 1e-08:
+        ratio, trips = ratio * ratio / (2.0 - ratio * ratio), trips + 1
+    sums = jnp.sum(jnp.abs(gram), axis=1, keepdims=True)
+    spread = jnp.max(sums, axis=0, keepdims=True)
+    start = 2.0 / (2.0 + spread)
+    inverse[...] = start * identity
+    residual[...] = (1.0 - start) * identity - start * gram
+
+    def grow(index, ratio):
+        square = ratio * ratio
+        scale = 2.0 / (2.0 - square)
+        both = exact_dot(jnp.concatenate([inverse[...], residual[...]], axis=0), residual[...])
+        inverse[...] = scale * (inverse[...] + both[:block])
+        residual[...] = (1.0 - scale) * identity + scale * both[block:]
+        return square / (2.0 - square)
+
+    lax.fori_loop(0, trips, grow, spread / (2.0 + spread))
+
+    def correct(index, carry):
+        guess = inverse[...]
+        residual[...] = identity - guess - exact_dot(gram, guess)
+        inverse[...] = guess + exact_dot(guess, residual[...])
+        return carry
+
+    lax.fori_loop(0, 2, correct, 0)
+
+
 def exchange_kernel(
-    count, length, matrix, rot_high, rot_low,
+    rows_all, count, length, matrix, rot_high, rot_low, out_keep, out_lead,
     lead, keep, lead_land, keep_land, total_keep, total_lead,
-    loaded, cross, norms, part, recv, mine, gathered, passed, gathered_lead,
-    load_sem, lead_send, lead_recv, keep_send, keep_recv,
+    cross, norms, part, recv, mine, gathered, passed, gathered_lead,
+    coupling, inverse, residual, high, low,
+    lead_send, lead_recv, keep_send, keep_recv,
     sum_send, sum_recv, all_send, all_recv, pass_send, pass_recv, more_send, more_recv, go_sem,
 ):
-    rows, cols = loaded.shape
+    rows, cols = matrix.shape
     block = cols // 2
     step = rows // CHUNKS
     me = lax.axis_index("rows")
@@ -221,16 +261,12 @@
     lead_peer, keep_peer = partners(position, length)
     core_peer = position + 1 - 2 * (position % 2)
     near = keep_peer == core_peer
+    even = position % 2 == 0
     left_leads = jnp.logical_or(position % 2 == 1, position == 0)
     signals = jnp.logical_and(position > 0, position < length - 1)
 
     def at(chunk):
         return pl.ds(pl.multiple_of(chunk * step, step), step)
-
-    def load(chunk):
-        return pltpu.make_async_copy(
-            matrix.at[at(chunk)], loaded.at[at(chunk)], load_sem.at[chunk]
-        )
 
     def send_lead(chunk):
         return pairs_copy(
@@ -244,15 +280,13 @@
             keep_send.at[chunk], keep_recv.at[chunk], keep_peer,
         )
 
-    def loop(low, high, do):
+    def loop(begin, end, do):
         def body(chunk, carry):
             do(chunk)
             return carry
 
-        lax.fori_loop(low, high, body, 0)
-
-    for chunk in range(CHUNKS):
-        load(chunk).start()
+        lax.fori_loop(begin, end, body, 0)
+
     barrier = pltpu.get_barrier_semaphore()
     for far in range(1, count):
         greet(barrier, "rows", lax.rem(me + far, count))
@@ -260,9 +294,8 @@
         greet(barrier, "pairs", peer)
     pl.semaphore_wait(barrier, count + 2)
 
-    def turn(chunk):
-        load(chunk).wait()
-        turned = dot_three(split(loaded[at(chunk), :]), (rot_high[...], rot_low[...]), 1)
+    def rotate(chunk):
+        turned = dot_three(split(matrix[at(chunk), :]), (rot_high[...], rot_low[...]), 1)
         left, right = turned[:, :block], turned[:, block:]
         lead[at(chunk), :] = jnp.where(left_leads, left, right)
         keep[at(chunk), :] = jnp.where(left_leads, right, left)
@@ -272,16 +305,11 @@
         def _():
             send_keep(chunk).start()
 
-    loop(0, CHUNKS, turn)
-    cross[...] = jnp.zeros_like(cross)
-    norms[...] = jnp.zeros_like(norms)
-
     def take(chunk):
         send_lead(chunk).wait_recv()
-        mine_rows, theirs = keep[at(chunk), :], keep_land[at(chunk), :]
-        cross[...] += dot_three(split(mine_rows), split(theirs), 0)
-        norms[0:1, :] += jnp.sum(mine_rows * mine_rows, axis=0, keepdims=True)
-        norms[1:2, :] += jnp.sum(theirs * theirs, axis=0, keepdims=True)
+        ours, theirs = keep[at(chunk), :], keep_land[at(chunk), :]
+        cross[...] += dot_three(split(ours), split(theirs), 0)
+        add_norms(norms, ours, theirs)
 
     def hand_over():
         loop(0, CHUNKS - 1, lambda chunk: send_lead(chunk).wait_send())
@@ -292,6 +320,30 @@
                 go_sem, inc=1, device_id={"pairs": core_peer}, device_id_type=MESH
             )
 
+    def prepare(total, flip, takes_first, own_out):
+        scales = unpack(total, coupling)
+        identity = identity_of(block)
+        couple(rows_all, scales, coupling, identity)
+        value = coupling[...]
+        coupling[...] = jnp.where(flip, value.T, value)
+        value = coupling[...]
+        invert_fixed(exact_dot(value, value, 1, 1), inverse, residual, identity)
+        straight = 2.0 * inverse[...] - identity
+        sign = jnp.where(takes_first, -2.0, 2.0)
+        crossed = sign * exact_dot(coupling[...], inverse[...], 0)
+        own = jnp.where(own_out, straight, crossed)
+        landed = jnp.where(own_out, crossed, straight)
+        high[0], low[0] = split(own)
+        high[1], low[1] = split(landed)
+
+    def finish(out, own, landed, chunk):
+        out[at(chunk), :] = dot_three(split(own[at(chunk), :]), (high[0], low[0]), 1) + dot_three(
+            split(landed[at(chunk), :]), (high[1], low[1]), 1
+        )
+
+    loop(0, CHUNKS, rotate)
+    cross[...] = jnp.zeros_like(cross)
+    norms[...] = jnp.zeros_like(norms)
     loop(0, CHUNKS - 1, take)
 
     @pl.when(jnp.logical_not(near))
@@ -310,47 +362,67 @@
     @pl.when(jnp.logical_not(near))
     def _():
         loop(EARLY, CHUNKS, lambda chunk: send_keep(chunk).start())
+        piece.wait_recv()
+        gather_start(count, passed, gathered_lead, more_send, more_recv)
 
     gather_finish(count, mine, gathered, total_keep, more)
+    prepare(
+        total_keep,
+        position != 1,
+        jnp.logical_and(jnp.logical_not(even), position != 1),
+        position == 1,
+    )
 
     @pl.when(near)
     def _():
         hand_over()
-
-    piece.wait_recv()
-    rest = gather_start(count, passed, gathered_lead, more_send, more_recv)
+        piece.wait_recv()
+        gather_start(count, passed, gathered_lead, more_send, more_recv)
+
+    loop(0, CHUNKS, lambda chunk: finish(out_keep, keep, keep_land, chunk))
+    rest = [
+        rows_copy(passed, gathered_lead.at[far], more_send.at[far], more_recv.at[far], lax.rem(me + far, count))
+        for far in range(1, count)
+    ]
     gather_finish(count, passed, gathered_lead, total_lead, rest)
+    prepare(
+        total_lead,
+        position == 0,
+        jnp.logical_or(even, position == length - 1),
+        position == 0,
+    )
+
+    def last(chunk):
+        send_keep(chunk).wait_recv()
+        finish(out_lead, lead, lead_land, chunk)
+
+    loop(0, CHUNKS, last)
     for copy in copies + more + rest + [piece]:
         copy.wait_send()
     send_lead(CHUNKS - 1).wait_send()
-    loop(0, CHUNKS, lambda chunk: send_keep(chunk).wait())
-
-
-def exchange(matrix, rotation, slot):
+    loop(0, CHUNKS, lambda chunk: send_keep(chunk).wait_send())
+
+
+def exchange(rows_all, matrix, rotation, slot):
     rows, cols = matrix.shape
     block = cols // 2
     count = lax.axis_size("rows")
     length = lax.axis_size("pairs")
     vmem = pl.BlockSpec(memory_space=pltpu.VMEM)
-    pieces = (count,) + slot
+    pieces = pltpu.VMEM((count,) + slot, F32)
     return pl.pallas_call(
-        functools.partial(exchange_kernel, count, length),
-        out_shape=[jax.ShapeDtypeStruct((rows, block), F32)] * 4
-        + [jax.ShapeDtypeStruct(pieces, F32)] * 2,
-        in_specs=[pl.BlockSpec(memory_space=pl.ANY), vmem, vmem],
-        out_specs=[vmem] * 6,
-        scratch_shapes=[
-            pltpu.VMEM((rows, cols), F32),
-            pltpu.VMEM((block, block), F32),
-            pltpu.VMEM((8, block), F32),
-            pltpu.VMEM(pieces, F32),
-            pltpu.VMEM(pieces, F32),
-            pltpu.VMEM(slot, F32),
-            pltpu.VMEM(pieces, F32),
-            pltpu.VMEM(slot, F32),
-            pltpu.VMEM(pieces, F32),
-        ]
-        + [DMA((CHUNKS,))] * 5
+        functools.partial(exchange_kernel, rows_all, count, length),
+        out_shape=[jax.ShapeDtypeStruct((rows, block), F32)] * 2,
+        in_specs=[vmem] * 3,
+        out_specs=[vmem] * 2,
+        scratch_shapes=[pltpu.VMEM((rows, block), F32)] * 4
+        + [pieces] * 2
+        + [pltpu.VMEM((block, block), F32), pltpu.VMEM((8, block // 2), F32)]
+        + [pieces] * 2
+        + [pltpu.VMEM(slot, F32), pieces, pltpu.VMEM(slot, F32), pieces]
+        + [pltpu.VMEM((block, block), F32)] * 3
+        + [pltpu.VMEM((2, block, block), BF16)] * 2
+        + [DMA((CHUNKS,))] * 4
         + [DMA((count,))] * 4
         + [DMA(()), DMA(())]
         + [DMA((count,))] * 2
@@ -446,106 +518,46 @@
     )(total)
 
 
-def final_kernel(
-    rows_all, place, lead, keep, lead_land, keep_land, total_keep, total_lead, out,
-    turns, inverses, residuals, high, low, staged, sems,
-):
+def store_kernel(keep, lead, out, sems):
     rows, block = lead.shape
-    step = rows // CHUNKS
-    position, length = place[0], place[1]
-    identity = identity_of(block)
-    couplings = [turns.at[0], turns.at[1]]
-    own_out = [position == 1, position == 0]
-    flips = [jnp.logical_not(own_out[0]), own_out[1]]
-    odd = position % 2 == 1
-    grams = []
-    for index, total in enumerate((total_keep, total_lead)):
-        norms = unpack(total, couplings[index])
-        couple(rows_all, norms, couplings[index], identity)
-        value = couplings[index][...]
-        couplings[index][...] = jnp.where(flips[index], value.T, value)
-        value = couplings[index][...]
-        grams.append(exact_dot(value, value, 1, 1))
-    invert(
-        grams,
-        [inverses.at[0], inverses.at[1]],
-        [residuals.at[0], residuals.at[1]],
-        identity,
-    )
-    first_slot = [odd, jnp.logical_not(odd)]
-    for index in range(2):
-        takes_first = jnp.where(
-            first_slot[index], position != 1, position == length - 1
-        )
-        inverse = inverses[index]
-        straight = 2.0 * inverse - identity
-        sign = jnp.where(takes_first, -2.0, 2.0)
-        crossed = sign * exact_dot(couplings[index][...], inverse, 0)
-        own = jnp.where(own_out[index], straight, crossed)
-        landed = jnp.where(own_out[index], crossed, straight)
-        for part, value in enumerate((own, landed)):
-            top, bottom = split(value)
-            high[index, part] = top
-            low[index, part] = bottom
-
-    def at(chunk):
-        return pl.ds(pl.multiple_of(chunk * step, step), step)
+    step = rows // STORES
+    odd = lax.axis_index("pairs") % 2
 
     def store(chunk, index):
-        column = jnp.where(first_slot[index], 0, block)
+        column = jnp.where(odd == index, block, 0)
+        at = pl.ds(chunk * step, step)
         return pltpu.make_async_copy(
-            staged.at[index, at(chunk)],
-            out.at[at(chunk), pl.ds(pl.multiple_of(column, block), block)],
+            (keep, lead)[index].at[at],
+            out.at[at, pl.ds(pl.multiple_of(column, block), block)],
             sems.at[index, chunk],
         )
 
-    def body(chunk, carry):
-        for index, (own, landed) in enumerate(((keep, keep_land), (lead, lead_land))):
-            staged[index, at(chunk), :] = dot_three(
-                split(own[at(chunk), :]), (high[index, 0], low[index, 0]), 1
-            ) + dot_three(split(landed[at(chunk), :]), (high[index, 1], low[index, 1]), 1)
-            store(chunk, index).start()
-        return carry
-
-    lax.fori_loop(0, CHUNKS, body, 0)
-
-    def drain(chunk, carry):
-        store(chunk, 0).wait()
-        store(chunk, 1).wait()
-        return carry
-
-    lax.fori_loop(0, CHUNKS, drain, 0)
-
-
-def final(rows_all, blocks, totals):
-    rows, block = blocks[0].shape
+    copies = [store(chunk, index) for chunk in range(STORES) for index in range(2)]
+    for copy in copies:
+        copy.start()
+    for copy in copies:
+        copy.wait()
+
+
+def store(keep, lead):
+    rows, block = lead.shape
     vmem = pl.BlockSpec(memory_space=pltpu.VMEM)
-    place = jnp.stack([lax.axis_index("pairs"), jnp.int32(lax.axis_size("pairs"))])
     return pl.pallas_call(
-        functools.partial(final_kernel, rows_all),
+        store_kernel,
         out_shape=jax.ShapeDtypeStruct((rows, 2 * block), F32),
-        in_specs=[pl.BlockSpec(memory_space=pltpu.SMEM)] + [vmem] * 6,
+        in_specs=[vmem] * 2,
         out_specs=pl.BlockSpec(memory_space=pl.ANY),
-        scratch_shapes=[
-            pltpu.VMEM((2, block, block), F32),
-            pltpu.VMEM((2, block, block), F32),
-            pltpu.VMEM((2, block, block), F32),
-            pltpu.VMEM((2, 2, block, block), BF16),
-            pltpu.VMEM((2, 2, block, block), BF16),
-            pltpu.VMEM((2, rows, block), F32),
-            DMA((2, CHUNKS)),
-        ],
-        name="final",
-        compiler_params=pltpu.CompilerParams(vmem_limit_bytes=32 * 2**20),
-    )(place, *blocks, *totals)
+        scratch_shapes=[DMA((2, STORES))],
+        name="store",
+        compiler_params=pltpu.CompilerParams(vmem_limit_bytes=16 * 2**20),
+    )(keep, lead)
 
 
 def shards(matrix):
     rows_all = matrix.shape[0] * lax.axis_size("rows")
-    total = products(matrix)
+    total, loaded = products(pltpu.with_memory_space_constraint(matrix, pltpu.HBM))
     rotation = rotation_of(total, rows_all)
-    moved = exchange(matrix, rotation, total.shape[1:])
-    return final(rows_all, moved[:4], moved[4:])
+    return store(*exchange(rows_all, loaded, rotation, total.shape[1:]))
 
 
 def solution(mesh):

time: 97.4 us -> 97.3 us (level)
  the two profiles are of different devices: /device:TPU:1 before, /device:TPU:31 now
where the time goes in v2:
time: 97.3 us; the launch traced here: 97.1 us
  Pallas kernels  97.1 us (100%)
    pallas_call x1, Pallas kernels, exchange(): pl.pallas_call(functools.partial(exchange_kernel, rows_all, count, length...  74.3 us
    pallas_call x1, Pallas kernels, products(): pl.pallas_call(functools.partial(products_kernel, count), out_shape=[jax....  15.2 us
    pallas_call x1, Pallas kernels, rotation_of(): pl.pallas_call(functools.partial(rotation_kernel, rows_all), out_shape=[j...  5.52 us
    pallas_call x1, Pallas kernels, store(): pl.pallas_call(store_kernel, out_shape=jax.ShapeDtypeStruct((rows, 2 * bl...  2.08 us

profile of v2, /device:TPU:31, one launch (start us, length us, event | category | flops | bytes accessed | tf_op | source)
XLA Modules:
  0.0 97.1 jit_solution(4337487833429159643)
XLA Ops:
  0.0 15.2 %products.1 = (f32[8,72,128]{2,1,0:T(8,128)S(1)}, f32[2048,512]{1,0:T(8,128)S(1)}) custom-call(f32[2048,512]{1,0:T(8,128)} %matrix.1), custom_call_target="tpu_custom_call" | custom-call | tf_op jit(solution)/shard_map/products/pallas_call | solution.py:192
  15.2 5.5 %rotation.1 = (bf16[512,512]{1,0:T(8,128)(2,1)S(1)}, bf16[512,512]{1,0:T(8,128)(2,1)S(1)}) custom-call(f32[8,72,128]{2,1,0:T(8,128)S(1)} %get-tuple-element.12.total), custom_call_target="tpu_custom_call" | custom-call | tf_op jit(solution)/shard_map/rotation/pallas_call | solution.py:510
  20.7 74.3 %exchange.1 = (f32[2048,256]{1,0:T(8,128)S(1)}, f32[2048,256]{1,0:T(8,128)S(1)}) custom-call(f32[2048,512]{1,0:T(8,128)S(1)} %get-tuple-element.11.matrix, bf16[512,512]{1,0:T(8,128)(2,1)S(1)} %get-tuple-element.13.rot_high, bf16[512,512]{1,0:T(8,128)(2,1)S(1)} %get-tuple-element.14.rot_low), custom_call_target="tpu_custom_call" | custom-call | tf_op jit(solution)/shard_map/exchange/pallas_call | solution.py:413
  95.1 2.1 %store.1 = f32[2048,512]{1,0:T(8,128)} custom-call(f32[2048,256]{1,0:T(8,128)S(1)} %get-tuple-element.15.keep, f32[2048,256]{1,0:T(8,128)S(1)} %get-tuple-element.16.lead), custom_call_target="tpu_custom_call" | custom-call | tf_op jit(solution)/shard_map/store/pallas_call | solution.py:545

commit v3 on v2

--- a/solution.py
+++ b/solution.py
@@ -7,8 +7,11 @@
 from jax.experimental.pallas import tpu as pltpu
 from jax.sharding import PartitionSpec as P
 
+LOADS = 4
 CHUNKS = 8
-EARLY = 4
+SENDS = 16
+EARLY = 6
+RELAY = 10
 STORES = 4
 F32 = jnp.float32
 BF16 = jnp.bfloat16
@@ -148,7 +151,7 @@
 def products_kernel(count, matrix, total, loaded, load_sem, cross, norms, part, recv, mine, gathered, *sems):
     rows, cols = loaded.shape
     block = cols // 2
-    step = rows // CHUNKS
+    step = rows // LOADS
 
     def at(chunk):
         return pl.ds(pl.multiple_of(chunk * step, step), step)
@@ -158,7 +161,7 @@
             matrix.at[at(chunk)], loaded.at[at(chunk)], load_sem.at[chunk]
         )
 
-    for chunk in range(CHUNKS):
+    for chunk in range(LOADS):
         load(chunk).start()
     barrier = pltpu.get_barrier_semaphore()
     me = lax.axis_index("rows")
@@ -174,7 +177,7 @@
         add_norms(norms, first, second)
         return carry
 
-    lax.fori_loop(0, CHUNKS, take, 0)
+    lax.fori_loop(0, LOADS, take, 0)
     pack(count, cross, norms, part)
     pl.semaphore_wait(barrier, count - 1)
     copies = scatter_sum(count, part, recv, mine, sems[0], sems[1])
@@ -198,7 +201,7 @@
         in_specs=[pl.BlockSpec(memory_space=pltpu.HBM)],
         out_specs=[pl.BlockSpec(memory_space=pltpu.VMEM)] * 2,
         scratch_shapes=[
-            DMA((CHUNKS,)),
+            DMA((LOADS,)),
             pltpu.VMEM((block, block), F32),
             pltpu.VMEM((8, block // 2), F32),
             pltpu.VMEM((count,) + slot, F32),
@@ -218,7 +221,7 @@
     block = identity.shape[0]
     largest = 0.25 * block * block
     ratio, trips = largest / (2.0 + largest), 0
-    while ratio > 1e-08:
+    while ratio > 0.01:
         ratio, trips = ratio * ratio / (2.0 - ratio * ratio), trips + 1
     sums = jnp.sum(jnp.abs(gram), axis=1, keepdims=True)
     spread = jnp.max(sums, axis=0, keepdims=True)
@@ -229,17 +232,18 @@
     def grow(index, ratio):
         square = ratio * ratio
         scale = 2.0 / (2.0 - square)
-        both = exact_dot(jnp.concatenate([inverse[...], residual[...]], axis=0), residual[...])
-        inverse[...] = scale * (inverse[...] + both[:block])
-        residual[...] = (1.0 - scale) * identity + scale * both[block:]
+        power = split(residual[...])
+        more = dot_three(split(inverse[...]), power, 1)
+        inverse[...] = scale * (inverse[...] + more)
+        residual[...] = (1.0 - scale) * identity + scale * dot_three(power, power, 1)
         return square / (2.0 - square)
 
     lax.fori_loop(0, trips, grow, spread / (2.0 + spread))
 
     def correct(index, carry):
         guess = inverse[...]
-        residual[...] = identity - guess - exact_dot(gram, guess)
-        inverse[...] = guess + exact_dot(guess, residual[...])
+        error = identity - guess - exact_dot(gram, guess)
+        inverse[...] = guess + dot_three(split(guess), split(error), 1)
         return carry
 
     lax.fori_loop(0, 2, correct, 0)
@@ -255,34 +259,36 @@
 ):
     rows, cols = matrix.shape
     block = cols // 2
-    step = rows // CHUNKS
+    step = rows // SENDS
+    group = SENDS // CHUNKS
     me = lax.axis_index("rows")
     position = lax.axis_index("pairs")
     lead_peer, keep_peer = partners(position, length)
     core_peer = position + 1 - 2 * (position % 2)
-    near = keep_peer == core_peer
+    near_keep = keep_peer == core_peer
+    near_lead = lead_peer == core_peer
     even = position % 2 == 0
     left_leads = jnp.logical_or(position % 2 == 1, position == 0)
     signals = jnp.logical_and(position > 0, position < length - 1)
 
-    def at(chunk):
-        return pl.ds(pl.multiple_of(chunk * step, step), step)
-
-    def send_lead(chunk):
+    def at(send, sends=1):
+        return pl.ds(pl.multiple_of(send * step, step), sends * step)
+
+    def send_lead(send):
         return pairs_copy(
-            lead.at[at(chunk)], keep_land.at[at(chunk)],
-            lead_send.at[chunk], lead_recv.at[chunk], lead_peer,
+            lead.at[at(send)], keep_land.at[at(send)],
+            lead_send.at[send], lead_recv.at[send], lead_peer,
         )
 
-    def send_keep(chunk):
+    def send_keep(send):
         return pairs_copy(
-            keep.at[at(chunk)], lead_land.at[at(chunk)],
-            keep_send.at[chunk], keep_recv.at[chunk], keep_peer,
+            keep.at[at(send)], lead_land.at[at(send)],
+            keep_send.at[send], keep_recv.at[send], keep_peer,
         )
 
     def loop(begin, end, do):
-        def body(chunk, carry):
-            do(chunk)
+        def body(index, carry):
+            do(index)
             return carry
 
         lax.fori_loop(begin, end, body, 0)
@@ -292,33 +298,45 @@
         greet(barrier, "rows", lax.rem(me + far, count))
     for peer in (lead_peer, keep_peer, core_peer):
         greet(barrier, "pairs", peer)
-    pl.semaphore_wait(barrier, count + 2)
-
-    def rotate(chunk):
-        turned = dot_three(split(matrix[at(chunk), :]), (rot_high[...], rot_low[...]), 1)
+
+    def turn(chunk):
+        where = at(chunk * group, group)
+        turned = dot_three(split(matrix[where, :]), (rot_high[...], rot_low[...]), 1)
         left, right = turned[:, :block], turned[:, block:]
-        lead[at(chunk), :] = jnp.where(left_leads, left, right)
-        keep[at(chunk), :] = jnp.where(left_leads, right, left)
-        send_lead(chunk).start()
-
-        @pl.when(near)
+        lead[where, :] = jnp.where(left_leads, left, right)
+        keep[where, :] = jnp.where(left_leads, right, left)
+
+    def send(chunk):
+        for offset in range(group):
+            send_lead(chunk * group + offset).start()
+
+        @pl.when(near_keep)
         def _():
-            send_keep(chunk).start()
-
-    def take(chunk):
-        send_lead(chunk).wait_recv()
-        ours, theirs = keep[at(chunk), :], keep_land[at(chunk), :]
+            for offset in range(group):
+                send_keep(chunk * group + offset).start()
+
+    def turn_and_send(chunk):
+        turn(chunk)
+        send(chunk)
+
+    def take(send):
+        send_lead(send).wait_recv()
+        ours, theirs = keep[at(send), :], keep_land[at(send), :]
         cross[...] += dot_three(split(ours), split(theirs), 0)
         add_norms(norms, ours, theirs)
 
     def hand_over():
-        loop(0, CHUNKS - 1, lambda chunk: send_lead(chunk).wait_send())
+        loop(0, SENDS - 1, lambda send: send_lead(send).wait_send())
 
         @pl.when(signals)
         def _():
             pl.semaphore_signal(
                 go_sem, inc=1, device_id={"pairs": core_peer}, device_id_type=MESH
             )
+
+    def relay():
+        pairs_copy(mine, passed, pass_send, pass_recv, keep_peer).wait_recv()
+        gather_start(count, passed, gathered_lead, more_send, more_recv)
 
     def prepare(total, flip, takes_first, own_out):
         scales = unpack(total, coupling)
@@ -337,70 +355,92 @@
         high[1], low[1] = split(landed)
 
     def finish(out, own, landed, chunk):
-        out[at(chunk), :] = dot_three(split(own[at(chunk), :]), (high[0], low[0]), 1) + dot_three(
-            split(landed[at(chunk), :]), (high[1], low[1]), 1
+        where = at(chunk * group, group)
+        out[where, :] = dot_three(split(own[where, :]), (high[0], low[0]), 1) + dot_three(
+            split(landed[where, :]), (high[1], low[1]), 1
         )
 
-    loop(0, CHUNKS, rotate)
+    def finish_lead():
+        gather_finish(count, passed, gathered_lead, total_lead, rest)
+        prepare(
+            total_lead,
+            position == 0,
+            jnp.logical_or(even, position == length - 1),
+            position == 0,
+        )
+
+        def last(chunk):
+            for offset in range(group):
+                send_keep(chunk * group + offset).wait_recv()
+            finish(out_lead, lead, lead_land, chunk)
+
+        loop(0, CHUNKS, last)
+
+    rest = [
+        rows_copy(
+            passed, gathered_lead.at[far], more_send.at[far], more_recv.at[far],
+            lax.rem(me + far, count),
+        )
+        for far in range(1, count)
+    ]
+    turn(0)
     cross[...] = jnp.zeros_like(cross)
     norms[...] = jnp.zeros_like(norms)
-    loop(0, CHUNKS - 1, take)
-
-    @pl.when(jnp.logical_not(near))
+    pl.semaphore_wait(barrier, count + 2)
+    send(0)
+    loop(1, CHUNKS, turn_and_send)
+    loop(0, RELAY, take)
+
+    @pl.when(near_lead)
+    def _():
+        relay()
+
+    loop(RELAY, SENDS - 1, take)
+
+    @pl.when(jnp.logical_not(near_keep))
     def _():
         hand_over()
         pl.semaphore_wait(go_sem, 1)
-        loop(0, EARLY, lambda chunk: send_keep(chunk).start())
-
-    take(CHUNKS - 1)
+        loop(0, EARLY, lambda send: send_keep(send).start())
+
+    take(SENDS - 1)
     pack(count, cross, norms, part)
     copies = scatter_sum(count, part, recv, mine, sum_send, sum_recv)
     piece = pairs_copy(mine, passed, pass_send, pass_recv, keep_peer)
     piece.start()
     more = gather_start(count, mine, gathered, all_send, all_recv)
 
-    @pl.when(jnp.logical_not(near))
+    @pl.when(jnp.logical_not(near_keep))
     def _():
-        loop(EARLY, CHUNKS, lambda chunk: send_keep(chunk).start())
-        piece.wait_recv()
-        gather_start(count, passed, gathered_lead, more_send, more_recv)
+        loop(EARLY, SENDS, lambda send: send_keep(send).start())
+
+    @pl.when(near_lead)
+    def _():
+        finish_lead()
 
     gather_finish(count, mine, gathered, total_keep, more)
+
+    @pl.when(near_keep)
+    def _():
+        hand_over()
+
     prepare(
         total_keep,
         position != 1,
         jnp.logical_and(jnp.logical_not(even), position != 1),
         position == 1,
     )
-
-    @pl.when(near)
+    loop(0, CHUNKS, lambda chunk: finish(out_keep, keep, keep_land, chunk))
+
+    @pl.when(jnp.logical_not(near_lead))
     def _():
-        hand_over()
-        piece.wait_recv()
-        gather_start(count, passed, gathered_lead, more_send, more_recv)
-
-    loop(0, CHUNKS, lambda chunk: finish(out_keep, keep, keep_land, chunk))
-    rest = [
-        rows_copy(passed, gathered_lead.at[far], more_send.at[far], more_recv.at[far], lax.rem(me + far, count))
-        for far in range(1, count)
-    ]
-    gather_finish(count, passed, gathered_lead, total_lead, rest)
-    prepare(
-        total_lead,
-        position == 0,
-        jnp.logical_or(even, position == length - 1),
-        position == 0,
-    )
-
-    def last(chunk):
-        send_keep(chunk).wait_recv()
-        finish(out_lead, lead, lead_land, chunk)
-
-    loop(0, CHUNKS, last)
+        relay()
+        finish_lead()
+
     for copy in copies + more + rest + [piece]:
         copy.wait_send()
-    send_lead(CHUNKS - 1).wait_send()
-    loop(0, CHUNKS, lambda chunk: send_keep(chunk).wait_send())
+    send_lead(SENDS - 1).wait_send()
+    loop(0, SENDS, lambda send: send_keep(send).wait_send())
 
 
 def exchange(rows_all, matrix, rotation, slot):
@@ -422,7 +462,7 @@
         + [pltpu.VMEM(slot, F32), pieces, pltpu.VMEM(slot, F32), pieces]
         + [pltpu.VMEM((block, block), F32)] * 3
         + [pltpu.VMEM((2, block, block), BF16)] * 2
-        + [DMA((CHUNKS,))] * 4
+        + [DMA((SENDS,))] * 4
         + [DMA((count,))] * 4
         + [DMA(()), DMA(())]
         + [DMA((count,))] * 2

time: 97.3 us -> 82.1 us (0.84)
  the two profiles are of different devices: /device:TPU:31 before, /device:TPU:1 now
where the time goes in v3:
time: 82.1 us; the launch traced here: 80.9 us
  Pallas kernels  80.9 us (99%)
    pallas_call x1, Pallas kernels, exchange(): pl.pallas_call(functools.partial(exchange_kernel, rows_all, count, length...  56.5 us
    pallas_call x1, Pallas kernels, products(): pl.pallas_call(functools.partial(products_kernel, count), out_shape=[jax....  16.8 us
    pallas_call x1, Pallas kernels, rotation_of(): pl.pallas_call(functools.partial(rotation_kernel, rows_all), out_shape=[j...  5.52 us
    pallas_call x1, Pallas kernels, store(): pl.pallas_call(store_kernel, out_shape=jax.ShapeDtypeStruct((rows, 2 * bl...  2.08 us

profile of v3, /device:TPU:1, one launch (start us, length us, event | category | flops | bytes accessed | tf_op | source)
XLA Modules:
  0.0 80.9 jit_solution(2089311800991467785)
XLA Ops:
  0.0 16.8 %products.1 = (f32[8,72,128]{2,1,0:T(8,128)S(1)}, f32[2048,512]{1,0:T(8,128)S(1)}) custom-call(f32[2048,512]{1,0:T(8,128)} %matrix.1), custom_call_target="tpu_custom_call" | custom-call | tf_op jit(solution)/shard_map/products/pallas_call | solution.py:195
  16.8 5.5 %rotation.1 = (bf16[512,512]{1,0:T(8,128)(2,1)S(1)}, bf16[512,512]{1,0:T(8,128)(2,1)S(1)}) custom-call(f32[8,72,128]{2,1,0:T(8,128)S(1)} %get-tuple-element.12.total), custom_call_target="tpu_custom_call" | custom-call | tf_op jit(solution)/shard_map/rotation/pallas_call | solution.py:550
  22.4 56.5 %exchange.1 = (f32[2048,256]{1,0:T(8,128)S(1)}, f32[2048,256]{1,0:T(8,128)S(1)}) custom-call(f32[2048,512]{1,0:T(8,128)S(1)} %get-tuple-element.11.matrix, bf16[512,512]{1,0:T(8,128)(2,1)S(1)} %get-tuple-element.13.rot_high, bf16[512,512]{1,0:T(8,128)(2,1)S(1)} %get-tuple-element.14.rot_low), custom_call_target="tpu_custom_call" | custom-call | tf_op jit(solution)/shard_map/exchange/pallas_call | solution.py:453
  78.8 2.1 %store.1 = f32[2048,512]{1,0:T(8,128)} custom-call(f32[2048,256]{1,0:T(8,128)S(1)} %get-tuple-element.15.keep, f32[2048,256]{1,0:T(8,128)S(1)} %get-tuple-element.16.lead), custom_call_target="tpu_custom_call" | custom-call | tf_op jit(solution)/shard_map/store/pallas_call | solution.py:585

commit v4 on v3

--- a/solution.py
+++ b/solution.py
@@ -11,7 +11,8 @@
 CHUNKS = 8
 SENDS = 16
 EARLY = 6
-RELAY = 10
+RAW = 6
+RAW_FIRST = 3
 STORES = 4
 F32 = jnp.float32
 BF16 = jnp.bfloat16
@@ -148,10 +149,22 @@
         total[lax.rem(me + count - far, count)] = gathered[far]
 
 
-def products_kernel(count, matrix, total, loaded, load_sem, cross, norms, part, recv, mine, gathered, *sems):
+def products_kernel(
+    count, length, matrix, total, loaded, raw, raw_piece,
+    load_sem, cross, norms, part, recv, mine, gathered,
+    sum_send, sum_recv, all_send, all_recv, raw_send, raw_recv, piece_send, piece_recv,
+):
     rows, cols = loaded.shape
     block = cols // 2
     step = rows // LOADS
+    send_rows = rows // SENDS
+    raw_start = rows - RAW * send_rows
+    me = lax.axis_index("rows")
+    position = lax.axis_index("pairs")
+    lead_peer, keep_peer = partners(position, length)
+    core_peer = position + 1 - 2 * (position % 2)
+    sends_raw = lead_peer != core_peer
+    takes_raw = keep_peer != core_peer
 
     def at(chunk):
         return pl.ds(pl.multiple_of(chunk * step, step), step)
@@ -161,14 +174,28 @@
             matrix.at[at(chunk)], loaded.at[at(chunk)], load_sem.at[chunk]
         )
 
+    def raw_copy(index):
+        return pairs_copy(
+            matrix.at[pl.ds(raw_start + index * send_rows, send_rows)],
+            raw.at[pl.ds(index * send_rows, send_rows)],
+            raw_send.at[index], raw_recv.at[index], lead_peer,
+        )
+
     for chunk in range(LOADS):
         load(chunk).start()
     barrier = pltpu.get_barrier_semaphore()
-    me = lax.axis_index("rows")
     for far in range(1, count):
         greet(barrier, "rows", lax.rem(me + far, count))
+    greet(barrier, "pairs", lead_peer)
+    greet(barrier, "pairs", keep_peer)
     cross[...] = jnp.zeros_like(cross)
     norms[...] = jnp.zeros_like(norms)
+    pl.semaphore_wait(barrier, count + 1)
+
+    @pl.when(sends_raw)
+    def _():
+        for index in range(RAW_FIRST):
+            raw_copy(index).start()
 
     def take(chunk, carry):
         load(chunk).wait()
@@ -179,27 +206,49 @@
 
     lax.fori_loop(0, LOADS, take, 0)
     pack(count, cross, norms, part)
-    pl.semaphore_wait(barrier, count - 1)
-    copies = scatter_sum(count, part, recv, mine, sems[0], sems[1])
-    more = gather_start(count, mine, gathered, sems[2], sems[3])
+    copies = scatter_sum(count, part, recv, mine, sum_send, sum_recv)
+    more = gather_start(count, mine, gathered, all_send, all_recv)
+    piece = pairs_copy(mine, raw_piece, piece_send, piece_recv, lead_peer)
+
+    @pl.when(sends_raw)
+    def _():
+        piece.start()
+        for index in range(RAW_FIRST, RAW):
+            raw_copy(index).start()
+
     gather_finish(count, mine, gathered, total, more)
     for copy in copies + more:
         copy.wait_send()
+
+    @pl.when(sends_raw)
+    def _():
+        piece.wait_send()
+        for index in range(RAW):
+            raw_copy(index).wait_send()
+
+    @pl.when(takes_raw)
+    def _():
+        piece.wait_recv()
+        for index in range(RAW):
+            raw_copy(index).wait_recv()
 
 
 def products(matrix):
     rows, cols = matrix.shape
     block = cols // 2
     count = lax.axis_size("rows")
+    length = lax.axis_size("pairs")
     slot = (2 * (block // count) + 8, block // 2)
     return pl.pallas_call(
-        functools.partial(products_kernel, count),
+        functools.partial(products_kernel, count, length),
         out_shape=[
             jax.ShapeDtypeStruct((count,) + slot, F32),
             jax.ShapeDtypeStruct((rows, cols), F32),
+            jax.ShapeDtypeStruct((RAW * (rows // SENDS), cols), F32),
+            jax.ShapeDtypeStruct(slot, F32),
         ],
         in_specs=[pl.BlockSpec(memory_space=pltpu.HBM)],
-        out_specs=[pl.BlockSpec(memory_space=pltpu.VMEM)] * 2,
+        out_specs=[pl.BlockSpec(memory_space=pltpu.VMEM)] * 4,
         scratch_shapes=[
             DMA((LOADS,)),
             pltpu.VMEM((block, block), F32),
@@ -209,7 +258,9 @@
             pltpu.VMEM(slot, F32),
             pltpu.VMEM((count,) + slot, F32),
         ]
-        + [DMA((count,))] * 4,
+        + [DMA((count,))] * 4
+        + [DMA((RAW,))] * 2
+        + [DMA(())] * 2,
         name="products",
         compiler_params=pltpu.CompilerParams(
             collective_id=0, has_side_effects=True, vmem_limit_bytes=24 * 2**20
@@ -250,12 +301,12 @@
 
 
 def exchange_kernel(
-    rows_all, count, length, matrix, rot_high, rot_low, out_keep, out_lead,
+    rows_all, count, length, matrix, rot_high, rot_low, raw, raw_piece, out_keep, out_lead,
     lead, keep, lead_land, keep_land, total_keep, total_lead,
-    cross, norms, part, recv, mine, gathered, passed, gathered_lead,
+    cross, norms, part, recv, mine, gathered, passed, gathered_lead, total_raw, gathered_raw,
     coupling, inverse, residual, high, low,
     lead_send, lead_recv, keep_send, keep_recv,
-    sum_send, sum_recv, all_send, all_recv, pass_send, pass_recv, more_send, more_recv, go_sem,
+    sum_send, sum_recv, all_send, all_recv, pass_send, pass_recv, more_send, more_recv, raw_send, raw_recv, go_sem,
 ):
     rows, cols = matrix.shape
     block = cols // 2
@@ -270,6 +321,8 @@
     even = position % 2 == 0
     left_leads = jnp.logical_or(position % 2 == 1, position == 0)
     signals = jnp.logical_and(position > 0, position < length - 1)
+    sent = jnp.where(near_lead, SENDS, SENDS - RAW)
+    landing = jnp.where(near_keep, SENDS, SENDS - RAW)
 
     def at(send, sends=1):
         return pl.ds(pl.multiple_of(send * step, step), sends * step)
@@ -308,7 +361,9 @@
 
     def send(chunk):
         for offset in range(group):
-            send_lead(chunk * group + offset).start()
+            @pl.when(chunk * group + offset < sent)
+            def _():
+                send_lead(chunk * group + offset).start()
 
         @pl.when(near_keep)
         def _():
@@ -319,14 +374,32 @@
         turn(chunk)
         send(chunk)
 
-    def take(send):
-        send_lead(send).wait_recv()
+    def multiply(send):
         ours, theirs = keep[at(send), :], keep_land[at(send), :]
         cross[...] += dot_three(split(ours), split(theirs), 0)
         add_norms(norms, ours, theirs)
 
+    def take(send):
+        send_lead(send).wait_recv()
+        multiply(send)
+
+    def turn_raw():
+        gather_finish(count, raw_piece, gathered_raw, total_raw, raw_copies)
+        left = jnp.logical_or(keep_peer % 2 == 1, keep_peer == 0)
+        prepare(total_raw, jnp.logical_not(left), left, left)
+
+        def body(index):
+            source = pl.ds(pl.multiple_of(index * step, step), step)
+            send = SENDS - RAW + index
+            keep_land[at(send), :] = dot_three(
+                split(raw[source, :block]), (high[0], low[0]), 1
+            ) + dot_three(split(raw[source, block:]), (high[1], low[1]), 1)
+            multiply(send)
+
+        loop(0, RAW, body)
+
     def hand_over():
-        loop(0, SENDS - 1, lambda send: send_lead(send).wait_send())
+        loop(0, sent - 1, lambda send: send_lead(send).wait_send())
 
         @pl.when(signals)
         def _():
@@ -383,19 +456,31 @@
         )
         for far in range(1, count)
     ]
+    raw_copies = [
+        rows_copy(
+            raw_piece, gathered_raw.at[far], raw_send.at[far], raw_recv.at[far],
+            lax.rem(me + far, count),
+        )
+        for far in range(1, count)
+    ]
     turn(0)
     cross[...] = jnp.zeros_like(cross)
     norms[...] = jnp.zeros_like(norms)
     pl.semaphore_wait(barrier, count + 2)
     send(0)
+
+    @pl.when(jnp.logical_not(near_keep))
+    def _():
+        for copy in raw_copies:
+            copy.start()
+
     loop(1, CHUNKS, turn_and_send)
-    loop(0, RELAY, take)
-
-    @pl.when(near_lead)
-    def _():
-        relay()
-
-    loop(RELAY, SENDS - 1, take)
+
+    @pl.when(jnp.logical_not(near_keep))
+    def _():
+        turn_raw()
+
+    loop(0, landing - 1, take)
 
     @pl.when(jnp.logical_not(near_keep))
     def _():
@@ -403,7 +488,11 @@
         pl.semaphore_wait(go_sem, 1)
         loop(0, EARLY, lambda send: send_keep(send).start())
 
-    take(SENDS - 1)
+    @pl.when(near_lead)
+    def _():
+        relay()
+
+    take(landing - 1)
     pack(count, cross, norms, part)
     copies = scatter_sum(count, part, recv, mine, sum_send, sum_recv)
     piece = pairs_copy(mine, passed, pass_send, pass_recv, keep_peer)
@@ -414,16 +503,15 @@
     def _():
         loop(EARLY, SENDS, lambda send: send_keep(send).start())
 
+    @pl.when(near_keep)
+    def _():
+        hand_over()
+
     @pl.when(near_lead)
     def _():
         finish_lead()
 
     gather_finish(count, mine, gathered, total_keep, more)
-
-    @pl.when(near_keep)
-    def _():
-        hand_over()
-
     prepare(
         total_keep,
         position != 1,
@@ -439,39 +527,47 @@
 
     for copy in copies + more + rest + [piece]:
         copy.wait_send()
-    send_lead(SENDS - 1).wait_send()
+    send_lead(sent - 1).wait_send()
+
+    @pl.when(jnp.logical_not(near_keep))
+    def _():
+        for copy in raw_copies:
+            copy.wait_send()
+
     loop(0, SENDS, lambda send: send_keep(send).wait_send())
 
 
-def exchange(rows_all, matrix, rotation, slot):
+def exchange(rows_all, matrix, rotation, raw, raw_piece):
     rows, cols = matrix.shape
     block = cols // 2
     count = lax.axis_size("rows")
     length = lax.axis_size("pairs")
     vmem = pl.BlockSpec(memory_space=pltpu.VMEM)
+    slot = raw_piece.shape
     pieces = pltpu.VMEM((count,) + slot, F32)
     return pl.pallas_call(
         functools.partial(exchange_kernel, rows_all, count, length),
         out_shape=[jax.ShapeDtypeStruct((rows, block), F32)] * 2,
-        in_specs=[vmem] * 3,
+        in_specs=[vmem] * 5,
         out_specs=[vmem] * 2,
         scratch_shapes=[pltpu.VMEM((rows, block), F32)] * 4
         + [pieces] * 2
         + [pltpu.VMEM((block, block), F32), pltpu.VMEM((8, block // 2), F32)]
         + [pieces] * 2
-        + [pltpu.VMEM(slot, F32), pieces, pltpu.VMEM(slot, F32), pieces]
+        + [pltpu.VMEM(slot, F32), pieces, pltpu.VMEM(slot, F32)]
+        + [pieces] * 3
         + [pltpu.VMEM((block, block), F32)] * 3
         + [pltpu.VMEM((2, block, block), BF16)] * 2
         + [DMA((SENDS,))] * 4
         + [DMA((count,))] * 4
         + [DMA(()), DMA(())]
-        + [DMA((count,))] * 2
+        + [DMA((count,))] * 4
         + [pltpu.SemaphoreType.REGULAR],
         name="exchange",
         compiler_params=pltpu.CompilerParams(
             collective_id=1, has_side_effects=True, vmem_limit_bytes=32 * 2**20
         ),
-    )(matrix, *rotation)
+    )(matrix, *rotation, raw, raw_piece)
 
 
 def identity_of(block):
@@ -595,9 +691,9 @@
 
 def shards(matrix):
     rows_all = matrix.shape[0] * lax.axis_size("rows")
-    total, loaded = products(pltpu.with_memory_space_constraint(matrix, pltpu.HBM))
+    total, loaded, raw, raw_piece = products(pltpu.with_memory_space_constraint(matrix, pltpu.HBM))
     rotation = rotation_of(total, rows_all)
-    return store(*exchange(rows_all, loaded, rotation, total.shape[1:]))
+    return store(*exchange(rows_all, loaded, rotation, raw, raw_piece))
 
 
 def solution(mesh):

time: 82.1 us -> 84.8 us (1.033)
  the two profiles are of different devices: /device:TPU:1 before, /device:TPU:0 now
where the time goes in v4:
time: 84.8 us; the launch traced here: 84.7 us
  Pallas kernels  84.6 us (100%)
    pallas_call x1, Pallas kernels, exchange(): pl.pallas_call(functools.partial(exchange_kernel, rows_all, count, length...  50.1 us
    pallas_call x1, Pallas kernels, products(): pl.pallas_call(functools.partial(products_kernel, count, length), out_sha...  27 us
    pallas_call x1, Pallas kernels, rotation_of(): pl.pallas_call(functools.partial(rotation_kernel, rows_all), out_shape=[j...  5.52 us
    pallas_call x1, Pallas kernels, store(): pl.pallas_call(store_kernel, out_shape=jax.ShapeDtypeStruct((rows, 2 * bl...  2.08 us

profile of v4, /device:TPU:0, one launch (start us, length us, event | category | flops | bytes accessed | tf_op | source)
XLA Modules:
  0.0 84.7 jit_solution(18105498049675917807)
XLA Ops:
  0.0 27.0 %products.1 = (f32[8,72,128]{2,1,0:T(8,128)S(1)}, f32[2048,512]{1,0:T(8,128)S(1)}, f32[768,512]{1,0:T(8,128)S(1)}, f32[72,128]{1,0:T(8,128)S(1)}) custom-call(f32[2048,512]{1,0:T(8,128)} %matrix.1), custom_call_target="tpu_custom_call" | custom-call | tf_op jit(solution)/shard_map/products/pallas_call | solution.py:242
  27.0 5.5 %rotation.1 = (bf16[512,512]{1,0:T(8,128)(2,1)S(1)}, bf16[512,512]{1,0:T(8,128)(2,1)S(1)}) custom-call(f32[8,72,128]{2,1,0:T(8,128)S(1)} %get-tuple-element.14.total), custom_call_target="tpu_custom_call" | custom-call | tf_op jit(solution)/shard_map/rotation/pallas_call | solution.py:646
  32.5 50.1 %exchange.1 = (f32[2048,256]{1,0:T(8,128)S(1)}, f32[2048,256]{1,0:T(8,128)S(1)}) custom-call(f32[2048,512]{1,0:T(8,128)S(1)} %get-tuple-element.13.matrix, bf16[512,512]{1,0:T(8,128)(2,1)S(1)} %get-tuple-element.15.rot_high, bf16[512,512]{1,0:T(8,128)(2,1)S(1)} %get-tuple-element.16.rot_low, f32[768,512]{1,0:T(8,128)S(1)} %get-tuple-element.17.raw, ...), custom_call_target="tpu_custom_call" | custom-call | tf_op jit(solution)/shard_map/exchange/pallas_call | solution.py:548
  82.6 2.1 %store.1 = f32[2048,512]{1,0:T(8,128)} custom-call(f32[2048,256]{1,0:T(8,128)S(1)} %get-tuple-element.19.keep, f32[2048,256]{1,0:T(8,128)S(1)} %get-tuple-element.20.lead), custom_call_target="tpu_custom_call" | custom-call | tf_op jit(solution)/shard_map/store/pallas_call | solution.py:681

commit v5 on v3

v5 whole, which is shorter than its diff:
```python
import functools

import jax
import jax.numpy as jnp
from jax import lax
from jax.experimental import pallas as pl
from jax.experimental.pallas import tpu as pltpu
from jax.sharding import PartitionSpec as P

LOADS = 4
CHUNKS = 8
SENDS = 16
OUTS = 4
EARLY = 6
RAW = 8
RAW_FIRST = 3
STORES = 4
F32 = jnp.float32
BF16 = jnp.bfloat16
MESH = pl.DeviceIdType.MESH
DMA = pltpu.SemaphoreType.DMA


def split(value):
    high = value.astype(BF16)
    return high, (value - high.astype(F32)).astype(BF16)


def dot_bf16(left, right, left_dim):
    return lax.dot_general(
        left, right, (((left_dim,), (0,)), ((), ())), preferred_element_type=F32
    )


def dot_three(left, right, left_dim):
    return (
        dot_bf16(left[0], right[1], left_dim)
        + dot_bf16(left[1], right[0], left_dim)
        + dot_bf16(left[0], right[0], left_dim)
    )


def exact_dot(left, right, left_dim=1, right_dim=0):
    return lax.dot_general(
        left,
        right,
        (((left_dim,), (right_dim,)), ((), ())),
        precision=lax.Precision.HIGHEST,
        preferred_element_type=F32,
    )


def rows_copy(src, dst, send, recv, peer):
    return pltpu.make_async_remote_copy(
        src_ref=src,
        dst_ref=dst,
        send_sem=send,
        recv_sem=recv,
        device_id={"rows": peer},
        device_id_type=MESH,
    )


def pairs_copy(src, dst, send, recv, peer):
    return pltpu.make_async_remote_copy(
        src_ref=src,
        dst_ref=dst,
        send_sem=send,
        recv_sem=recv,
        device_id={"pairs": peer},
        device_id_type=MESH,
    )


def greet(barrier, axis, peer):
    pl.semaphore_signal(barrier, inc=1, device_id={axis: peer}, device_id_type=MESH)


def partners(position, length):
    even = position % 2 == 0
    down = jnp.where(position == 0, 1, position - 2)
    up = jnp.where(position == length - 1, length - 2, position + 2)
    lead = jnp.where(even, down, up)
    down = jnp.where(position == 1, 0, position - 2)
    up = jnp.where(position == length - 2, length - 1, position + 2)
    keep = jnp.where(even, up, down)
    return lead, keep


def add_norms(norms, first, second):
    half = norms.shape[1]
    for row, value in ((0, first), (1, second)):
        sums = jnp.sum(value * value, axis=0, keepdims=True)
        norms[row : row + 1, :] += sums[:, :half]
        norms[row + 4 : row + 5, :] += sums[:, half:]


def pack(count, cross, norms, part):
    block = cross.shape[0]
    share = block // count
    half = block // 2
    for slot in range(count):
        part[slot, :share, :] = cross[slot * share : (slot + 1) * share, :half]
        part[slot, share : 2 * share, :] = cross[slot * share : (slot + 1) * share, half:]
        part[slot, 2 * share : 2 * share + 8, :] = norms[...]


def unpack(total, cross):
    count, depth, half = total.shape
    share = (depth - 8) // 2
    for slot in range(count):
        cross[slot * share : (slot + 1) * share, :half] = total[slot, :share, :]
        cross[slot * share : (slot + 1) * share, half:] = total[slot, share : 2 * share, :]
    norms = total[0, 2 * share :, :]
    return jnp.concatenate([norms[0:4], norms[4:8]], axis=1)


def scatter_sum(count, part, recv, mine, send_sems, recv_sems):
    me = lax.axis_index("rows")
    copies = []
    for far in range(1, count):
        peer = lax.rem(me + far, count)
        copy = rows_copy(part.at[peer], recv.at[far], send_sems.at[far], recv_sems.at[far], peer)
        copy.start()
        copies.append(copy)
    acc = part[me]
    for far in range(1, count):
        copies[far - 1].wait_recv()
        acc = acc + recv[far]
    mine[...] = acc
    return copies


def gather_start(count, mine, gathered, send_sems, recv_sems):
    me = lax.axis_index("rows")
    copies = []
    for far in range(1, count):
        peer = lax.rem(me + far, count)
        copy = rows_copy(mine, gathered.at[far], send_sems.at[far], recv_sems.at[far], peer)
        copy.start()
        copies.append(copy)
    return copies


def gather_finish(count, mine, gathered, total, copies):
    me = lax.axis_index("rows")
    total[me] = mine[...]
    for far in range(1, count):
        copies[far - 1].wait_recv()
        total[lax.rem(me + count - far, count)] = gathered[far]


def invert_fixed(gram, inverse, residual, identity):
    block = identity.shape[0]
    largest = 0.25 * block * block
    ratio, trips = largest / (2.0 + largest), 0
    while ratio > 0.05:
        ratio, trips = ratio * ratio / (2.0 - ratio * ratio), trips + 1
    sums = jnp.sum(jnp.abs(gram), axis=1, keepdims=True)
    spread = jnp.max(sums, axis=0, keepdims=True)
    start = 2.0 / (2.0 + spread)
    inverse[...] = start * identity
    residual[...] = (1.0 - start) * identity - start * gram

    def grow(index, ratio):
        square = ratio * ratio
        scale = 2.0 / (2.0 - square)
        power = split(residual[...])
        more = dot_three(split(inverse[...]), power, 1)
        inverse[...] = scale * (inverse[...] + more)
        residual[...] = (1.0 - scale) * identity + scale * dot_three(power, power, 1)
        return square / (2.0 - square)

    lax.fori_loop(0, trips, grow, spread / (2.0 + spread))

    def correct(index, carry):
        guess = inverse[...]
        error = identity - guess - exact_dot(gram, guess)
        inverse[...] = guess + dot_three(split(guess), split(error), 1)
        return carry

    lax.fori_loop(0, 2, correct, 0)


def identity_of(block):
    row = lax.broadcasted_iota(jnp.int32, (block, block), 0)
    col = lax.broadcasted_iota(jnp.int32, (block, block), 1)
    return jnp.where(row == col, 1.0, 0.0).astype(F32)


def couple(rows_all, norms, cross, identity):
    scales = lax.rsqrt(norms / rows_all + 1e-06)
    scale_first = jnp.sum(identity * scales[0:1, :], axis=1, keepdims=True)
    cross[...] = 0.5 * cross[...] * scale_first * scales[1:2, :] / rows_all


def sweep_kernel(
    rows_all, count, length, matrix, out_keep, out_lead,
    loaded, raw, lead, keep, lead_land, keep_land,
    cross, norms, part, recv, mine, gathered, total,
    cross_two, norms_two, part_two, recv_two, mine_two, gathered_two, total_keep,
    passed, gathered_lead, total_lead, raw_piece, gathered_raw, total_raw,
    coupling, inverse, residual, high, low, rot_high, rot_low,
    load_sem, lead_send, lead_recv, keep_send, keep_recv, raw_send, raw_recv,
    sum_send, sum_recv, all_send, all_recv, sum_two_send, sum_two_recv, all_two_send, all_two_recv,
    more_send, more_recv, rest_send, rest_recv,
    pass_send, pass_recv, piece_send, piece_recv, go_sem,
):
    rows, cols = loaded.shape
    block = cols // 2
    step = rows // SENDS
    group = SENDS // CHUNKS
    me = lax.axis_index("rows")
    position = lax.axis_index("pairs")
    lead_peer, keep_peer = partners(position, length)
    core_peer = position + 1 - 2 * (position % 2)
    near_keep = keep_peer == core_peer
    near_lead = lead_peer == core_peer
    far_keep = jnp.logical_not(near_keep)
    far_lead = jnp.logical_not(near_lead)
    even = position % 2 == 0
    left_leads = jnp.logical_or(position % 2 == 1, position == 0)
    signals = jnp.logical_and(position > 0, position < length - 1)
    sent = jnp.where(near_lead, SENDS, SENDS - RAW)
    landing = jnp.where(near_keep, SENDS, SENDS - RAW)

    def at(send, sends=1):
        return pl.ds(pl.multiple_of(send * step, step), sends * step)

    def load(chunk):
        where = at(chunk * (SENDS // LOADS), SENDS // LOADS)
        return pltpu.make_async_copy(matrix.at[where], loaded.at[where], load_sem.at[chunk])

    def send_raw(index):
        return pairs_copy(
            matrix.at[at(SENDS - RAW + index)], raw.at[at(index)],
            raw_send.at[index], raw_recv.at[index], lead_peer,
        )

    def send_lead(send):
        return pairs_copy(
            lead.at[at(send)], keep_land.at[at(send)],
            lead_send.at[send], lead_recv.at[send], lead_peer,
        )

    def send_keep(send):
        return pairs_copy(
            keep.at[at(send)], lead_land.at[at(send)],
            keep_send.at[send], keep_recv.at[send], keep_peer,
        )

    def loop(begin, end, do):
        def body(index, carry):
            do(index)
            return carry

        lax.fori_loop(begin, end, body, 0)

    def relay_copies(source, target, send_sems, recv_sems):
        return [
            rows_copy(
                source, target.at[far], send_sems.at[far], recv_sems.at[far],
                lax.rem(me + far, count),
            )
            for far in range(1, count)
        ]

    piece = pairs_copy(mine, raw_piece, piece_send, piece_recv, lead_peer)
    piece_two = pairs_copy(mine_two, passed, pass_send, pass_recv, keep_peer)
    raw_copies = relay_copies(raw_piece, gathered_raw, rest_send, rest_recv)
    lead_copies = relay_copies(passed, gathered_lead, more_send, more_recv)

    def turn(chunk):
        where = at(chunk * group, group)
        turned = dot_three(split(loaded[where, :]), (rot_high[...], rot_low[...]), 1)
        left, right = turned[:, :block], turned[:, block:]
        lead[where, :] = jnp.where(left_leads, left, right)
        keep[where, :] = jnp.where(left_leads, right, left)
        for offset in range(group):
            send = chunk * group + offset

            @pl.when(send < sent)
            def _():
                send_lead(send).start()

            @pl.when(near_keep)
            def _():
                send_keep(send).start()

    def multiply(chunk):
        where = at(chunk * group, group)
        ours, theirs = keep[where, :], keep_land[where, :]
        cross_two[...] += dot_three(split(ours), split(theirs), 0)
        add_norms(norms_two, ours, theirs)

    def take(chunk):
        for offset in range(group):
            send_lead(chunk * group + offset).wait_recv()
        multiply(chunk)

    def hand_over():
        loop(0, sent - 1, lambda send: send_lead(send).wait_send())

        @pl.when(signals)
        def _():
            pl.semaphore_signal(
                go_sem, inc=1, device_id={"pairs": core_peer}, device_id_type=MESH
            )

    def relay_lead():
        piece_two.wait_recv()
        for copy in lead_copies:
            copy.start()

    def couple_and_invert(sums, flip):
        scales = unpack(sums, coupling)
        identity = identity_of(block)
        couple(rows_all, scales, coupling, identity)
        if flip is not None:
            value = coupling[...]
            coupling[...] = jnp.where(flip, value.T, value)
        value = coupling[...]
        invert_fixed(exact_dot(value, value, 1, 1), inverse, residual, identity)
        return 2.0 * inverse[...] - identity, identity

    def prepare_both():
        straight, identity = couple_and_invert(total, None)
        upper = exact_dot(inverse[...], coupling[...])
        lower = exact_dot(coupling[...], upper, 0)
        parts = (
            (0, 0, straight),
            (0, 1, 2.0 * upper),
            (1, 0, -2.0 * upper.T),
            (1, 1, identity - 2.0 * lower),
        )
        for down, across, value in parts:
            where = (pl.ds(down * block, block), pl.ds(across * block, block))
            rot_high[where], rot_low[where] = split(value)

    def prepare(sums, flip, takes_first, own_out):
        straight, identity = couple_and_invert(sums, flip)
        sign = jnp.where(takes_first, -2.0, 2.0)
        crossed = sign * exact_dot(coupling[...], inverse[...], 0)
        own = jnp.where(own_out, straight, crossed)
        landed = jnp.where(own_out, crossed, straight)
        high[0], low[0] = split(own)
        high[1], low[1] = split(landed)

    def turn_raw():
        gather_finish(count, raw_piece, gathered_raw, total_raw, raw_copies)
        left = jnp.logical_or(keep_peer % 2 == 1, keep_peer == 0)
        prepare(total_raw, jnp.logical_not(left), left, left)

        def body(chunk):
            for offset in range(group):
                send_raw(chunk * group + offset).wait_recv()
            source = at(chunk * group, group)
            keep_land[at(SENDS - RAW + chunk * group, group), :] = dot_three(
                split(raw[source, :block]), (high[0], low[0]), 1
            ) + dot_three(split(raw[source, block:]), (high[1], low[1]), 1)
            multiply(CHUNKS - RAW // group + chunk)

        loop(0, RAW // group, body)

    def finish(out, own, landed, chunk):
        where = at(chunk * (SENDS // OUTS), SENDS // OUTS)
        out[where, :] = dot_three(split(own[where, :]), (high[0], low[0]), 1) + dot_three(
            split(landed[where, :]), (high[1], low[1]), 1
        )

    def finish_lead():
        gather_finish(count, passed, gathered_lead, total_lead, lead_copies)
        prepare(
            total_lead,
            position == 0,
            jnp.logical_or(even, position == length - 1),
            position == 0,
        )

        def last(chunk):
            for offset in range(SENDS // OUTS):
                send_keep(chunk * (SENDS // OUTS) + offset).wait_recv()
            finish(out_lead, lead, lead_land, chunk)

        loop(0, OUTS, last)

    for chunk in range(LOADS):
        load(chunk).start()
    barrier = pltpu.get_barrier_semaphore()
    for far in range(1, count):
        greet(barrier, "rows", lax.rem(me + far, count))
    for peer in (lead_peer, keep_peer, core_peer):
        greet(barrier, "pairs", peer)
    for ref in (cross, norms, cross_two, norms_two):
        ref[...] = jnp.zeros_like(ref)
    pl.semaphore_wait(barrier, count + 2)

    @pl.when(far_lead)
    def _():
        loop(0, RAW_FIRST, lambda index: send_raw(index).start())

    def take_first(chunk):
        where = at(chunk * (SENDS // LOADS), SENDS // LOADS)
        load(chunk).wait()
        first, second = loaded[where, :block], loaded[where, block:]
        cross[...] += dot_three(split(first), split(second), 0)
        add_norms(norms, first, second)

    loop(0, LOADS, take_first)
    pack(count, cross, norms, part)
    sums = scatter_sum(count, part, recv, mine, sum_send, sum_recv)

    @pl.when(far_lead)
    def _():
        piece.start()
        loop(RAW_FIRST, RAW, lambda index: send_raw(index).start())

    alls = gather_start(count, mine, gathered, all_send, all_recv)

    @pl.when(far_keep)
    def _():
        piece.wait_recv()
        for copy in raw_copies:
            copy.start()

    gather_finish(count, mine, gathered, total, alls)
    prepare_both()
    loop(0, CHUNKS, turn)

    @pl.when(far_keep)
    def _():
        turn_raw()

    loop(0, landing // group - 1, take)

    @pl.when(far_keep)
    def _():
        hand_over()
        pl.semaphore_wait(go_sem, 1)
        loop(0, EARLY, lambda send: send_keep(send).start())

    @pl.when(near_lead)
    def _():
        relay_lead()

    take(landing // group - 1)
    pack(count, cross_two, norms_two, part_two)
    sums += scatter_sum(count, part_two, recv_two, mine_two, sum_two_send, sum_two_recv)
    piece_two.start()
    alls_two = gather_start(count, mine_two, gathered_two, all_two_send, all_two_recv)

    @pl.when(far_keep)
    def _():
        loop(EARLY, SENDS, lambda send: send_keep(send).start())

    @pl.when(near_keep)
    def _():
        hand_over()

    @pl.when(near_lead)
    def _():
        finish_lead()

    gather_finish(count, mine_two, gathered_two, total_keep, alls_two)
    prepare(
        total_keep,
        position != 1,
        jnp.logical_and(jnp.logical_not(even), position != 1),
        position == 1,
    )
    loop(0, OUTS, lambda chunk: finish(out_keep, keep, keep_land, chunk))

    @pl.when(far_lead)
    def _():
        relay_lead()
        finish_lead()

    for copy in sums + alls + alls_two + lead_copies + [piece_two]:
        copy.wait_send()
    send_lead(sent - 1).wait_send()

    @pl.when(far_keep)
    def _():
        for copy in raw_copies:
            copy.wait_send()

    @pl.when(far_lead)
    def _():
        piece.wait_send()
        loop(0, RAW, lambda index: send_raw(index).wait_send())

    loop(0, SENDS, lambda send: send_keep(send).wait_send())


def sweep(matrix):
    rows, cols = matrix.shape
    block = cols // 2
    count = lax.axis_size("rows")
    length = lax.axis_size("pairs")
    shape = (2 * (block // count) + 8, block // 2)
    slot, slots = pltpu.VMEM(shape, F32), pltpu.VMEM((count,) + shape, F32)
    square = pltpu.VMEM((block, block), F32)
    sums = [square, pltpu.VMEM((8, block // 2), F32), slots, slots, slot, slots, slots]
    vmem = pl.BlockSpec(memory_space=pltpu.VMEM)
    return pl.pallas_call(
        functools.partial(sweep_kernel, rows * count, count, length),
        out_shape=[jax.ShapeDtypeStruct((rows, block), F32)] * 2,
        in_specs=[pl.BlockSpec(memory_space=pltpu.HBM)],
        out_specs=[vmem] * 2,
        scratch_shapes=[pltpu.VMEM((rows, cols), F32)]
        + [pltpu.VMEM((RAW * (rows // SENDS), cols), F32)]
        + [pltpu.VMEM((rows, block), F32)] * 4
        + sums * 2
        + [slot, slots, slots] * 2
        + [square] * 3
        + [pltpu.VMEM((2, block, block), BF16)] * 2
        + [pltpu.VMEM((cols, cols), BF16)] * 2
        + [DMA((LOADS,))]
        + [DMA((SENDS,))] * 4
        + [DMA((RAW,))] * 2
        + [DMA((count,))] * 12
        + [DMA(())] * 4
        + [pltpu.SemaphoreType.REGULAR],
        name="sweep",
        compiler_params=pltpu.CompilerParams(
            collective_id=0, has_side_effects=True, vmem_limit_bytes=40 * 2**20
        ),
    )(pltpu.with_memory_space_constraint(matrix, pltpu.HBM))


def store_kernel(keep, lead, out, sems):
    rows, block = lead.shape
    step = rows // STORES
    odd = lax.axis_index("pairs") % 2

    def store(chunk, index):
        column = jnp.where(odd == index, block, 0)
        at = pl.ds(chunk * step, step)
        return pltpu.make_async_copy(
            (keep, lead)[index].at[at],
            out.at[at, pl.ds(pl.multiple_of(column, block), block)],
            sems.at[index, chunk],
        )

    copies = [store(chunk, index) for chunk in range(STORES) for index in range(2)]
    for copy in copies:
        copy.start()
    for copy in copies:
        copy.wait()


def store(keep, lead):
    rows, block = lead.shape
    vmem = pl.BlockSpec(memory_space=pltpu.VMEM)
    return pl.pallas_call(
        store_kernel,
        out_shape=jax.ShapeDtypeStruct((rows, 2 * block), F32),
        in_specs=[vmem] * 2,
        out_specs=pl.BlockSpec(memory_space=pl.ANY),
        scratch_shapes=[DMA((2, STORES))],
        name="store",
        compiler_params=pltpu.CompilerParams(vmem_limit_bytes=16 * 2**20),
    )(keep, lead)


def shards(matrix):
    return store(*sweep(matrix))


def solution(mesh):
    return jax.shard_map(
        shards,
        mesh=mesh,
        in_specs=(P("rows", "pairs"),),
        out_specs=P("rows", "pairs"),
        check_vma=False,
    )
```

time: 82.1 us -> 78.3 us (0.954)
  Pallas kernels: 80.9 us -> 76.9 us
    pallas_call x3 -> x1, Pallas kernels: 78.8 us -> 74.8 us  [sweep(): pl.pallas_call(functools.partial(sweep_kernel, rows * count, count, lengt...]
where the time goes in v5:
time: 78.3 us; the launch traced here: 77.1 us
  Pallas kernels  76.9 us (98%)
    pallas_call x1, Pallas kernels, sweep(): pl.pallas_call(functools.partial(sweep_kernel, rows * count, count, lengt...  74.8 us
    pallas_call x1, Pallas kernels, store(): pl.pallas_call(store_kernel, out_shape=jax.ShapeDtypeStruct((rows, 2 * bl...  2.08 us

profile of v5, /device:TPU:1, one launch (start us, length us, event | category | flops | bytes accessed | tf_op | source)
XLA Modules:
  0.0 77.1 jit_solution(16818170341550793971)
XLA Ops:
  0.0 74.8 %sweep.1 = (f32[2048,256]{1,0:T(8,128)S(1)}, f32[2048,256]{1,0:T(8,128)S(1)}) custom-call(f32[2048,512]{1,0:T(8,128)} %matrix.1), custom_call_target="tpu_custom_call" | custom-call | tf_op jit(solution)/shard_map/sweep/pallas_call | solution.py:505
  74.9 2.1 %store.1 = f32[2048,512]{1,0:T(8,128)} custom-call(f32[2048,256]{1,0:T(8,128)S(1)} %get-tuple-element.7.keep, f32[2048,256]{1,0:T(8,128)S(1)} %get-tuple-element.8.lead), custom_call_target="tpu_custom_call" | custom-call | tf_op jit(solution)/shard_map/store/pallas_call | solution.py:555

commit v6 on v5

--- a/solution.py
+++ b/solution.py
@@ -11,10 +11,9 @@
 CHUNKS = 8
 SENDS = 16
 OUTS = 4
-EARLY = 6
+EARLY = 5
 RAW = 8
 RAW_FIRST = 3
-STORES = 4
 F32 = jnp.float32
 BF16 = jnp.bfloat16
 MESH = pl.DeviceIdType.MESH
@@ -115,7 +114,7 @@
     return jnp.concatenate([norms[0:4], norms[4:8]], axis=1)
 
 
-def scatter_sum(count, part, recv, mine, send_sems, recv_sems):
+def scatter_start(count, part, recv, send_sems, recv_sems):
     me = lax.axis_index("rows")
     copies = []
     for far in range(1, count):
@@ -123,12 +122,15 @@
         copy = rows_copy(part.at[peer], recv.at[far], send_sems.at[far], recv_sems.at[far], peer)
         copy.start()
         copies.append(copy)
-    acc = part[me]
+    return copies
+
+
+def scatter_finish(count, part, recv, mine, copies):
+    acc = part[lax.axis_index("rows")]
     for far in range(1, count):
         copies[far - 1].wait_recv()
         acc = acc + recv[far]
     mine[...] = acc
-    return copies
 
 
 def gather_start(count, mine, gathered, send_sems, recv_sems):
@@ -154,7 +156,7 @@
     block = identity.shape[0]
     largest = 0.25 * block * block
     ratio, trips = largest / (2.0 + largest), 0
-    while ratio > 0.05:
+    while ratio > 0.01:
         ratio, trips = ratio * ratio / (2.0 - ratio * ratio), trips + 1
     sums = jnp.sum(jnp.abs(gram), axis=1, keepdims=True)
     spread = jnp.max(sums, axis=0, keepdims=True)
@@ -173,13 +175,9 @@
 
     lax.fori_loop(0, trips, grow, spread / (2.0 + spread))
 
-    def correct(index, carry):
-        guess = inverse[...]
-        error = identity - guess - exact_dot(gram, guess)
-        inverse[...] = guess + dot_three(split(guess), split(error), 1)
-        return carry
-
-    lax.fori_loop(0, 2, correct, 0)
+    guess = inverse[...]
+    error = identity - guess - exact_dot(gram, guess)
+    inverse[...] = guess + dot_three(split(guess), split(error), 1)
 
 
 def identity_of(block):
@@ -194,17 +192,23 @@
     cross[...] = 0.5 * cross[...] * scale_first * scales[1:2, :] / rows_all
 
 
+def two_blocks(own, landed, high, low, place):
+    return dot_three(split(own), (high[place, 0], low[place, 0]), 1) + dot_three(
+        split(landed), (high[place, 1], low[place, 1]), 1
+    )
+
+
 def sweep_kernel(
-    rows_all, count, length, matrix, out_keep, out_lead,
-    loaded, raw, lead, keep, lead_land, keep_land,
+    rows_all, count, length, matrix, out, lead, keep, lead_land, keep_land, high, low,
+    loaded, raw,
     cross, norms, part, recv, mine, gathered, total,
     cross_two, norms_two, part_two, recv_two, mine_two, gathered_two, total_keep,
     passed, gathered_lead, total_lead, raw_piece, gathered_raw, total_raw,
-    coupling, inverse, residual, high, low, rot_high, rot_low,
+    coupling, inverse, residual, rot_high, rot_low,
     load_sem, lead_send, lead_recv, keep_send, keep_recv, raw_send, raw_recv,
     sum_send, sum_recv, all_send, all_recv, sum_two_send, sum_two_recv, all_two_send, all_two_recv,
     more_send, more_recv, rest_send, rest_recv,
-    pass_send, pass_recv, piece_send, piece_recv, go_sem,
+    pass_send, pass_recv, piece_send, piece_recv, totals_send, totals_recv,
 ):
     rows, cols = loaded.shape
     block = cols // 2
@@ -220,9 +224,8 @@
     far_lead = jnp.logical_not(near_lead)
     even = position % 2 == 0
     left_leads = jnp.logical_or(position % 2 == 1, position == 0)
-    signals = jnp.logical_and(position > 0, position < length - 1)
     sent = jnp.where(near_lead, SENDS, SENDS - RAW)
-    landing = jnp.where(near_keep, SENDS, SENDS - RAW)
+    landing = SENDS - RAW
 
     def at(send, sends=1):
         return pl.ds(pl.multiple_of(send * step, step), sends * step)
@@ -267,6 +270,7 @@
 
     piece = pairs_copy(mine, raw_piece, piece_send, piece_recv, lead_peer)
     piece_two = pairs_copy(mine_two, passed, pass_send, pass_recv, keep_peer)
+    totals = pairs_copy(total_keep, total_lead, totals_send, totals_recv, keep_peer)
     raw_copies = relay_copies(raw_piece, gathered_raw, rest_send, rest_recv)
     lead_copies = relay_copies(passed, gathered_lead, more_send, more_recv)
 
@@ -297,20 +301,6 @@
         for offset in range(group):
             send_lead(chunk * group + offset).wait_recv()
         multiply(chunk)
-
-    def hand_over():
-        loop(0, sent - 1, lambda send: send_lead(send).wait_send())
-
-        @pl.when(signals)
-        def _():
-            pl.semaphore_signal(
-                go_sem, inc=1, device_id={"pairs": core_peer}, device_id_type=MESH
-            )
-
-    def relay_lead():
-        piece_two.wait_recv()
-        for copy in lead_copies:
-            copy.start()
 
     def couple_and_invert(sums, flip):
         scales = unpack(sums, coupling)
@@ -337,52 +327,46 @@
             where = (pl.ds(down * block, block), pl.ds(across * block, block))
             rot_high[where], rot_low[where] = split(value)
 
-    def prepare(sums, flip, takes_first, own_out):
+    def prepare(place, sums, flip, takes_first, own_out):
         straight, identity = couple_and_invert(sums, flip)
         sign = jnp.where(takes_first, -2.0, 2.0)
-        crossed = sign * exact_dot(coupling[...], inverse[...], 0)
+        crossed = sign * dot_three(split(coupling[...]), split(inverse[...]), 0)
         own = jnp.where(own_out, straight, crossed)
         landed = jnp.where(own_out, crossed, straight)
-        high[0], low[0] = split(own)
-        high[1], low[1] = split(landed)
+        high[place, 0], low[place, 0] = split(own)
+        high[place, 1], low[place, 1] = split(landed)
 
     def turn_raw():
         gather_finish(count, raw_piece, gathered_raw, total_raw, raw_copies)
         left = jnp.logical_or(keep_peer % 2 == 1, keep_peer == 0)
-        prepare(total_raw, jnp.logical_not(left), left, left)
+        prepare(0, total_raw, jnp.logical_not(left), left, left)
+        loop(0, RAW, lambda index: send_raw(index).wait_recv())
 
         def body(chunk):
-            for offset in range(group):
-                send_raw(chunk * group + offset).wait_recv()
             source = at(chunk * group, group)
-            keep_land[at(SENDS - RAW + chunk * group, group), :] = dot_three(
-                split(raw[source, :block]), (high[0], low[0]), 1
-            ) + dot_three(split(raw[source, block:]), (high[1], low[1]), 1)
-            multiply(CHUNKS - RAW // group + chunk)
+            keep_land[at(landing + chunk * group, group), :] = dot_three(
+                split(raw[source, :block]), (high[0, 0], low[0, 0]), 1
+            ) + dot_three(split(raw[source, block:]), (high[0, 1], low[0, 1]), 1)
+            multiply(landing // group + chunk)
 
         loop(0, RAW // group, body)
 
-    def finish(out, own, landed, chunk):
-        where = at(chunk * (SENDS // OUTS), SENDS // OUTS)
-        out[where, :] = dot_three(split(own[where, :]), (high[0], low[0]), 1) + dot_three(
-            split(landed[where, :]), (high[1], low[1]), 1
-        )
-
-    def finish_lead():
-        gather_finish(count, passed, gathered_lead, total_lead, lead_copies)
+    def prepare_lead(place):
         prepare(
+            place,
             total_lead,
             position == 0,
             jnp.logical_or(even, position == length - 1),
             position == 0,
         )
-
-        def last(chunk):
-            for offset in range(SENDS // OUTS):
-                send_keep(chunk * (SENDS // OUTS) + offset).wait_recv()
-            finish(out_lead, lead, lead_land, chunk)
-
-        loop(0, OUTS, last)
+        loop(0, SENDS, lambda send: send_keep(send).wait_recv())
+
+    def finish(own, landed):
+        def body(chunk):
+            where = at(chunk * (SENDS // OUTS), SENDS // OUTS)
+            out[where, :] = two_blocks(own[where, :], landed[where, :], high, low, 0)
+
+        loop(0, OUTS, body)
 
     for chunk in range(LOADS):
         load(chunk).start()
@@ -393,11 +377,6 @@
         greet(barrier, "pairs", peer)
     for ref in (cross, norms, cross_two, norms_two):
         ref[...] = jnp.zeros_like(ref)
-    pl.semaphore_wait(barrier, count + 2)
-
-    @pl.when(far_lead)
-    def _():
-        loop(0, RAW_FIRST, lambda index: send_raw(index).start())
 
     def take_first(chunk):
         where = at(chunk * (SENDS // LOADS), SENDS // LOADS)
@@ -407,8 +386,15 @@
         add_norms(norms, first, second)
 
     loop(0, LOADS, take_first)
+    pl.semaphore_wait(barrier, count + 2)
+
+    @pl.when(far_lead)
+    def _():
+        loop(0, RAW_FIRST, lambda index: send_raw(index).start())
+
     pack(count, cross, norms, part)
-    sums = scatter_sum(count, part, recv, mine, sum_send, sum_recv)
+    sums = scatter_start(count, part, recv, sum_send, sum_recv)
+    scatter_finish(count, part, recv, mine, sums)
 
     @pl.when(far_lead)
     def _():
@@ -416,6 +402,7 @@
         loop(RAW_FIRST, RAW, lambda index: send_raw(index).start())
 
     alls = gather_start(count, mine, gathered, all_send, all_recv)
+    gather_finish(count, mine, gathered, total, alls)
 
     @pl.when(far_keep)
     def _():
@@ -423,7 +410,6 @@
         for copy in raw_copies:
             copy.start()
 
-    gather_finish(count, mine, gathered, total, alls)
     prepare_both()
     loop(0, CHUNKS, turn)
 
@@ -431,53 +417,76 @@
     def _():
         turn_raw()
 
-    loop(0, landing // group - 1, take)
-
     @pl.when(far_keep)
     def _():
-        hand_over()
-        pl.semaphore_wait(go_sem, 1)
+        loop(0, landing // group - 1, take)
+        send_lead(landing - group).wait_recv()
         loop(0, EARLY, lambda send: send_keep(send).start())
+        for offset in range(1, group):
+            send_lead(landing - group + offset).wait_recv()
+        multiply(landing // group - 1)
+
+    @pl.when(near_keep)
+    def _():
+        loop(0, CHUNKS, take)
+
+    pack(count, cross_two, norms_two, part_two)
+    sums_two = scatter_start(count, part_two, recv_two, sum_two_send, sum_two_recv)
+    scatter_finish(count, part_two, recv_two, mine_two, sums_two)
+
+    @pl.when(far_keep)
+    def _():
+        piece_two.start()
+
+    alls_two = gather_start(count, mine_two, gathered_two, all_two_send, all_two_recv)
+
+    @pl.when(far_keep)
+    def _():
+        loop(EARLY, SENDS, lambda send: send_keep(send).start())
 
     @pl.when(near_lead)
     def _():
-        relay_lead()
-
-    take(landing // group - 1)
-    pack(count, cross_two, norms_two, part_two)
-    sums += scatter_sum(count, part_two, recv_two, mine_two, sum_two_send, sum_two_recv)
-    piece_two.start()
-    alls_two = gather_start(count, mine_two, gathered_two, all_two_send, all_two_recv)
-
-    @pl.when(far_keep)
-    def _():
-        loop(EARLY, SENDS, lambda send: send_keep(send).start())
+        totals.wait_recv()
+        prepare_lead(0)
+        finish(lead, lead_land)
+
+    gather_finish(count, mine_two, gathered_two, total_keep, alls_two)
 
     @pl.when(near_keep)
     def _():
-        hand_over()
-
-    @pl.when(near_lead)
-    def _():
-        finish_lead()
-
-    gather_finish(count, mine_two, gathered_two, total_keep, alls_two)
+        totals.start()
+
     prepare(
+        jnp.where(near_lead, 1, 0),
         total_keep,
         position != 1,
         jnp.logical_and(jnp.logical_not(even), position != 1),
         position == 1,
     )
-    loop(0, OUTS, lambda chunk: finish(out_keep, keep, keep_land, chunk))
 
     @pl.when(far_lead)
     def _():
-        relay_lead()
-        finish_lead()
-
-    for copy in sums + alls + alls_two + lead_copies + [piece_two]:
+        finish(keep, keep_land)
+        piece_two.wait_recv()
+        for copy in lead_copies:
+            copy.start()
+        gather_finish(count, passed, gathered_lead, total_lead, lead_copies)
+        prepare_lead(1)
+        for copy in lead_copies:
+            copy.wait_send()
+
+    for copy in sums + alls + sums_two + alls_two:
         copy.wait_send()
-    send_lead(sent - 1).wait_send()
+
+    @pl.when(near_keep)
+    def _():
+        totals.wait_send()
+
+    @pl.when(far_keep)
+    def _():
+        piece_two.wait_send()
+
+    loop(0, sent, lambda send: send_lead(send).wait_send())
 
     @pl.when(far_keep)
     def _():
@@ -504,67 +513,91 @@
     vmem = pl.BlockSpec(memory_space=pltpu.VMEM)
     return pl.pallas_call(
         functools.partial(sweep_kernel, rows * count, count, length),
-        out_shape=[jax.ShapeDtypeStruct((rows, block), F32)] * 2,
+        out_shape=[jax.ShapeDtypeStruct((rows, block), F32)] * 5
+        + [jax.ShapeDtypeStruct((2, 2, block, block), BF16)] * 2,
         in_specs=[pl.BlockSpec(memory_space=pltpu.HBM)],
-        out_specs=[vmem] * 2,
+        out_specs=[vmem] * 7,
         scratch_shapes=[pltpu.VMEM((rows, cols), F32)]
         + [pltpu.VMEM((RAW * (rows // SENDS), cols), F32)]
-        + [pltpu.VMEM((rows, block), F32)] * 4
         + sums * 2
         + [slot, slots, slots] * 2
         + [square] * 3
-        + [pltpu.VMEM((2, block, block), BF16)] * 2
         + [pltpu.VMEM((cols, cols), BF16)] * 2
         + [DMA((LOADS,))]
         + [DMA((SENDS,))] * 4
         + [DMA((RAW,))] * 2
         + [DMA((count,))] * 12
-        + [DMA(())] * 4
-        + [pltpu.SemaphoreType.REGULAR],
+        + [DMA(())] * 6,
         name="sweep",
         compiler_params=pltpu.CompilerParams(
-            collective_id=0, has_side_effects=True, vmem_limit_bytes=40 * 2**20
+            collective_id=0, has_side_effects=True, vmem_limit_bytes=24 * 2**20
         ),
     )(pltpu.with_memory_space_constraint(matrix, pltpu.HBM))
 
 
-def store_kernel(keep, lead, out, sems):
+def final_kernel(length, done, lead, keep, lead_land, keep_land, high, low, out, staged, sems):
     rows, block = lead.shape
-    step = rows // STORES
-    odd = lax.axis_index("pairs") % 2
-
-    def store(chunk, index):
-        column = jnp.where(odd == index, block, 0)
-        at = pl.ds(chunk * step, step)
+    step = rows // OUTS
+    position = lax.axis_index("pairs")
+    near_lead = jnp.logical_or(position == 0, position == length - 1)
+    even = position % 2 == 0
+
+    def store(chunk, source, takes_lead, sem):
+        column = jnp.where(takes_lead == even, 0, block)
+        where = pl.ds(pl.multiple_of(chunk * step, step), step)
         return pltpu.make_async_copy(
-            (keep, lead)[index].at[at],
-            out.at[at, pl.ds(pl.multiple_of(column, block), block)],
-            sems.at[index, chunk],
+            source.at[where],
+            out.at[where, pl.ds(pl.multiple_of(column, block), block)],
+            sems.at[sem, chunk],
         )
 
-    copies = [store(chunk, index) for chunk in range(STORES) for index in range(2)]
-    for copy in copies:
-        copy.start()
-    for copy in copies:
-        copy.wait()
-
-
-def store(keep, lead):
-    rows, block = lead.shape
-    vmem = pl.BlockSpec(memory_space=pltpu.VMEM)
+    def loop(do):
+        def body(chunk, carry):
+            do(chunk)
+            return carry
+
+        lax.fori_loop(0, OUTS, body, 0)
+
+    loop(lambda chunk: store(chunk, done, near_lead, 0).start())
+
+    def finish(own, landed):
+        def body(chunk):
+            where = pl.ds(pl.multiple_of(chunk * step, step), step)
+            staged[where, :] = two_blocks(own[where, :], landed[where, :], high, low, 1)
+            store(chunk, staged, jnp.logical_not(near_lead), 1).start()
+
+        loop(body)
+
+    @pl.when(near_lead)
+    def _():
+        finish(keep, keep_land)
+
+    @pl.when(jnp.logical_not(near_lead))
+    def _():
+        finish(lead, lead_land)
+
+    def drain(chunk):
+        store(chunk, done, near_lead, 0).wait()
+        store(chunk, staged, near_lead, 1).wait()
+
+    loop(drain)
+
+
+def final(done, *blocks):
+    rows, block = done.shape
     return pl.pallas_call(
-        store_kernel,
+        functools.partial(final_kernel, lax.axis_size("pairs")),
         out_shape=jax.ShapeDtypeStruct((rows, 2 * block), F32),
-        in_specs=[vmem] * 2,
+        in_specs=[pl.BlockSpec(memory_space=pltpu.VMEM)] * 7,
         out_specs=pl.BlockSpec(memory_space=pl.ANY),
-        scratch_shapes=[DMA((2, STORES))],
-        name="store",
+        scratch_shapes=[pltpu.VMEM((rows, block), F32), DMA((2, OUTS))],
+        name="final",
         compiler_params=pltpu.CompilerParams(vmem_limit_bytes=16 * 2**20),
-    )(keep, lead)
+    )(done, *blocks)
 
 
 def shards(matrix):
-    return store(*sweep(matrix))
+    return final(*sweep(matrix))
 
 
 def solution(mesh):

time: 78.3 us -> 73.5 us (0.939)
  the two profiles are of different devices: /device:TPU:1 before, /device:TPU:0 now
where the time goes in v6:
time: 73.5 us; the launch traced here: 73.4 us
  Pallas kernels  73.2 us (100%)
    pallas_call x1, Pallas kernels, sweep(): pl.pallas_call(functools.partial(sweep_kernel, rows * count, count, lengt...  70 us
    pallas_call x1, Pallas kernels, final(): pl.pallas_call(functools.partial(final_kernel, lax.axis_size('pairs')), o...  3.25 us

profile of v6, /device:TPU:0, one launch (start us, length us, event | category | flops | bytes accessed | tf_op | source)
XLA Modules:
  0.0 73.4 jit_solution(14398157236517119475)
XLA Ops:
  0.0 70.0 %sweep.1 = (f32[2048,256]{1,0:T(8,128)S(1)}, f32[2048,256]{1,0:T(8,128)S(1)}, f32[2048,256]{1,0:T(8,128)S(1)}, f32[2048,256]{1,0:T(8,128)S(1)}, f32[2048,256]{1,...) custom-call(f32[2048,512]{1,0:T(8,128)} %matrix.1), custom_call_target="tpu_custom_call" | custom-call | tf_op jit(solution)/shard_map/sweep/pallas_call | solution.py:514
  70.0 3.2 %final.1 = f32[2048,512]{1,0:T(8,128)} custom-call(f32[2048,256]{1,0:T(8,128)S(1)} %get-tuple-element.12.done, f32[2048,256]{1,0:T(8,128)S(1)} %get-tuple-element.13.lead, f32[2048,256]{1,0:T(8,128)S(1)} %get-tuple-element.14.keep, f32[2048,256]{1,0:T(8,128)S(1)} %get-tuple-element.15.lead_land, f32[2048,256]{1,0:T(8,128)S(1)} %get-tuple-element.16.keep_land, ...), custom_call_target="tpu_custom_call" | custom-call | tf_op jit(solution)/shard_map/final/pallas_call | solution.py:588

commit v7 on v6

--- a/solution.py
+++ b/solution.py
@@ -11,7 +11,7 @@
 CHUNKS = 8
 SENDS = 16
 OUTS = 4
-EARLY = 5
+EARLY = 7
 RAW = 8
 RAW_FIRST = 3
 F32 = jnp.float32
@@ -91,7 +91,7 @@
     for row, value in ((0, first), (1, second)):
         sums = jnp.sum(value * value, axis=0, keepdims=True)
         norms[row : row + 1, :] += sums[:, :half]
-        norms[row + 4 : row + 5, :] += sums[:, half:]
+        norms[row + 2 : row + 3, :] += sums[:, half:]
 
 
 def pack(count, cross, norms, part):
@@ -101,17 +101,17 @@
     for slot in range(count):
         part[slot, :share, :] = cross[slot * share : (slot + 1) * share, :half]
         part[slot, share : 2 * share, :] = cross[slot * share : (slot + 1) * share, half:]
-        part[slot, 2 * share : 2 * share + 8, :] = norms[...]
+        part[slot, 2 * share :, :] = norms[...]
 
 
 def unpack(total, cross):
     count, depth, half = total.shape
-    share = (depth - 8) // 2
+    share = (depth - 4) // 2
     for slot in range(count):
         cross[slot * share : (slot + 1) * share, :half] = total[slot, :share, :]
         cross[slot * share : (slot + 1) * share, half:] = total[slot, share : 2 * share, :]
     norms = total[0, 2 * share :, :]
-    return jnp.concatenate([norms[0:4], norms[4:8]], axis=1)
+    return jnp.concatenate([norms[0:2], norms[2:4]], axis=1)
 
 
 def scatter_start(count, part, recv, send_sems, recv_sems):
@@ -208,7 +208,7 @@
     load_sem, lead_send, lead_recv, keep_send, keep_recv, raw_send, raw_recv,
     sum_send, sum_recv, all_send, all_recv, sum_two_send, sum_two_recv, all_two_send, all_two_recv,
     more_send, more_recv, rest_send, rest_recv,
-    pass_send, pass_recv, piece_send, piece_recv, totals_send, totals_recv,
+    pass_send, pass_recv, piece_send, piece_recv, totals_send, totals_recv, go_sem,
 ):
     rows, cols = loaded.shape
     block = cols // 2
@@ -226,6 +226,7 @@
     left_leads = jnp.logical_or(position % 2 == 1, position == 0)
     sent = jnp.where(near_lead, SENDS, SENDS - RAW)
     landing = SENDS - RAW
+    signals = jnp.logical_and(position > 0, position < length - 1)
 
     def at(send, sends=1):
         return pl.ds(pl.multiple_of(send * step, step), sends * step)
@@ -301,6 +302,15 @@
         for offset in range(group):
             send_lead(chunk * group + offset).wait_recv()
         multiply(chunk)
+
+    def hand_over():
+        loop(0, sent, lambda send: send_lead(send).wait_send())
+
+        @pl.when(signals)
+        def _():
+            pl.semaphore_signal(
+                go_sem, inc=1, device_id={"pairs": core_peer}, device_id_type=MESH
+            )
 
     def couple_and_invert(sums, flip):
         scales = unpack(sums, coupling)
@@ -420,11 +430,10 @@
     @pl.when(far_keep)
     def _():
         loop(0, landing // group - 1, take)
-        send_lead(landing - group).wait_recv()
+        hand_over()
+        pl.semaphore_wait(go_sem, 1)
         loop(0, EARLY, lambda send: send_keep(send).start())
-        for offset in range(1, group):
-            send_lead(landing - group + offset).wait_recv()
-        multiply(landing // group - 1)
+        take(landing // group - 1)
 
     @pl.when(near_keep)
     def _():
@@ -432,6 +441,11 @@
 
     pack(count, cross_two, norms_two, part_two)
     sums_two = scatter_start(count, part_two, recv_two, sum_two_send, sum_two_recv)
+
+    @pl.when(near_keep)
+    def _():
+        hand_over()
+
     scatter_finish(count, part_two, recv_two, mine_two, sums_two)
 
     @pl.when(far_keep)
@@ -466,10 +480,10 @@
 
     @pl.when(far_lead)
     def _():
-        finish(keep, keep_land)
         piece_two.wait_recv()
         for copy in lead_copies:
             copy.start()
+        finish(keep, keep_land)
         gather_finish(count, passed, gathered_lead, total_lead, lead_copies)
         prepare_lead(1)
         for copy in lead_copies:
@@ -486,7 +500,6 @@
     def _():
         piece_two.wait_send()
 
-    loop(0, sent, lambda send: send_lead(send).wait_send())
 
     @pl.when(far_keep)
     def _():
@@ -506,10 +519,10 @@
     block = cols // 2
     count = lax.axis_size("rows")
     length = lax.axis_size("pairs")
-    shape = (2 * (block // count) + 8, block // 2)
+    shape = (2 * (block // count) + 4, block // 2)
     slot, slots = pltpu.VMEM(shape, F32), pltpu.VMEM((count,) + shape, F32)
     square = pltpu.VMEM((block, block), F32)
-    sums = [square, pltpu.VMEM((8, block // 2), F32), slots, slots, slot, slots, slots]
+    sums = [square, pltpu.VMEM((4, block // 2), F32), slots, slots, slot, slots, slots]
     vmem = pl.BlockSpec(memory_space=pltpu.VMEM)
     return pl.pallas_call(
         functools.partial(sweep_kernel, rows * count, count, length),
@@ -527,7 +540,8 @@
         + [DMA((SENDS,))] * 4
         + [DMA((RAW,))] * 2
         + [DMA((count,))] * 12
-        + [DMA(())] * 6,
+        + [DMA(())] * 6
+        + [pltpu.SemaphoreType.REGULAR],
         name="sweep",
         compiler_params=pltpu.CompilerParams(
             collective_id=0, has_side_effects=True, vmem_limit_bytes=24 * 2**20

time: 73.5 us -> 71.9 us (0.978)
  the two profiles are of different devices: /device:TPU:0 before, /device:TPU:1 now
where the time goes in v7:
time: 71.9 us; the launch traced here: 71.7 us
  Pallas kernels  71.5 us (99%)
    pallas_call x1, Pallas kernels, sweep(): pl.pallas_call(functools.partial(sweep_kernel, rows * count, count, lengt...  68.3 us
    pallas_call x1, Pallas kernels, final(): pl.pallas_call(functools.partial(final_kernel, lax.axis_size('pairs')), o...  3.24 us

profile of v7, /device:TPU:1, one launch (start us, length us, event | category | flops | bytes accessed | tf_op | source)
XLA Modules:
  0.0 71.7 jit_solution(5653072384649611127)
XLA Ops:
  0.0 68.3 %sweep.1 = (f32[2048,256]{1,0:T(8,128)S(1)}, f32[2048,256]{1,0:T(8,128)S(1)}, f32[2048,256]{1,0:T(8,128)S(1)}, f32[2048,256]{1,0:T(8,128)S(1)}, f32[2048,256]{1,...) custom-call(f32[2048,512]{1,0:T(8,128)} %matrix.1), custom_call_target="tpu_custom_call" | custom-call | tf_op jit(solution)/shard_map/sweep/pallas_call | solution.py:527
  68.3 3.2 %final.1 = f32[2048,512]{1,0:T(8,128)} custom-call(f32[2048,256]{1,0:T(8,128)S(1)} %get-tuple-element.12.done, f32[2048,256]{1,0:T(8,128)S(1)} %get-tuple-element.13.lead, f32[2048,256]{1,0:T(8,128)S(1)} %get-tuple-element.14.keep, f32[2048,256]{1,0:T(8,128)S(1)} %get-tuple-element.15.lead_land, f32[2048,256]{1,0:T(8,128)S(1)} %get-tuple-element.16.keep_land, ...), custom_call_target="tpu_custom_call" | custom-call | tf_op jit(solution)/shard_map/final/pallas_call | solution.py:602

commit v8 on v7

--- a/solution.py
+++ b/solution.py
@@ -11,7 +11,7 @@
 CHUNKS = 8
 SENDS = 16
 OUTS = 4
-EARLY = 7
+EARLY = 6
 RAW = 8
 RAW_FIRST = 3
 F32 = jnp.float32
@@ -237,7 +237,7 @@
 
     def send_raw(index):
         return pairs_copy(
-            matrix.at[at(SENDS - RAW + index)], raw.at[at(index)],
+            loaded.at[at(SENDS - RAW + index)], raw.at[at(index)],
             raw_send.at[index], raw_recv.at[index], lead_peer,
         )
 
@@ -369,7 +369,6 @@
             jnp.logical_or(even, position == length - 1),
             position == 0,
         )
-        loop(0, SENDS, lambda send: send_keep(send).wait_recv())
 
     def finish(own, landed):
         def body(chunk):
@@ -462,6 +461,7 @@
     def _():
         totals.wait_recv()
         prepare_lead(0)
+        loop(0, SENDS, lambda send: send_keep(send).wait_recv())
         finish(lead, lead_land)
 
     gather_finish(count, mine_two, gathered_two, total_keep, alls_two)
@@ -469,6 +469,12 @@
     @pl.when(near_keep)
     def _():
         totals.start()
+
+    @pl.when(far_lead)
+    def _():
+        piece_two.wait_recv()
+        for copy in lead_copies:
+            copy.start()
 
     prepare(
         jnp.where(near_lead, 1, 0),
@@ -480,12 +486,10 @@
 
     @pl.when(far_lead)
     def _():
-        piece_two.wait_recv()
-        for copy in lead_copies:
-            copy.start()
-        finish(keep, keep_land)
         gather_finish(count, passed, gathered_lead, total_lead, lead_copies)
         prepare_lead(1)
+        finish(keep, keep_land)
+        loop(0, SENDS, lambda send: send_keep(send).wait_recv())
         for copy in lead_copies:
             copy.wait_send()
 

time: 71.9 us -> 71.6 us (level)
  no operation moved by 1% of the time
where the time goes in v8:
time: 71.6 us; the launch traced here: 71.5 us
  Pallas kernels  71.3 us (100%)
    pallas_call x1, Pallas kernels, sweep(): pl.pallas_call(functools.partial(sweep_kernel, rows * count, count, lengt...  68.1 us
    pallas_call x1, Pallas kernels, final(): pl.pallas_call(functools.partial(final_kernel, lax.axis_size('pairs')), o...  3.24 us

profile of v8, /device:TPU:1, one launch (start us, length us, event | category | flops | bytes accessed | tf_op | source)
XLA Modules:
  0.0 71.5 jit_solution(9797740174811327676)
XLA Ops:
  0.0 68.1 %sweep.1 = (f32[2048,256]{1,0:T(8,128)S(1)}, f32[2048,256]{1,0:T(8,128)S(1)}, f32[2048,256]{1,0:T(8,128)S(1)}, f32[2048,256]{1,0:T(8,128)S(1)}, f32[2048,256]{1,...) custom-call(f32[2048,512]{1,0:T(8,128)} %matrix.1), custom_call_target="tpu_custom_call" | custom-call | tf_op jit(solution)/shard_map/sweep/pallas_call | solution.py:531
  68.1 3.2 %final.1 = f32[2048,512]{1,0:T(8,128)} custom-call(f32[2048,256]{1,0:T(8,128)S(1)} %get-tuple-element.12.done, f32[2048,256]{1,0:T(8,128)S(1)} %get-tuple-element.13.lead, f32[2048,256]{1,0:T(8,128)S(1)} %get-tuple-element.14.keep, f32[2048,256]{1,0:T(8,128)S(1)} %get-tuple-element.15.lead_land, f32[2048,256]{1,0:T(8,128)S(1)} %get-tuple-element.16.keep_land, ...), custom_call_target="tpu_custom_call" | custom-call | tf_op jit(solution)/shard_map/final/pallas_call | solution.py:606

commit v9 on v8

--- a/solution.py
+++ b/solution.py
@@ -10,7 +10,7 @@
 LOADS = 4
 CHUNKS = 8
 SENDS = 16
-OUTS = 4
+OUTS = 2
 EARLY = 6
 RAW = 8
 RAW_FIRST = 3

time: 71.6 us -> 71.4 us (level)
  no operation moved by 1% of the time
where the time goes in v9:
time: 71.4 us; the launch traced here: 71.3 us
  Pallas kernels  71.1 us (100%)
    pallas_call x1, Pallas kernels, sweep(): pl.pallas_call(functools.partial(sweep_kernel, rows * count, count, lengt...  68.1 us
    pallas_call x1, Pallas kernels, final(): pl.pallas_call(functools.partial(final_kernel, lax.axis_size('pairs')), o...  3.02 us

profile of v9, /device:TPU:1, one launch (start us, length us, event | category | flops | bytes accessed | tf_op | source)
XLA Modules:
  0.0 71.3 jit_solution(10228541032952054790)
XLA Ops:
  0.0 68.1 %sweep.1 = (f32[2048,256]{1,0:T(8,128)S(1)}, f32[2048,256]{1,0:T(8,128)S(1)}, f32[2048,256]{1,0:T(8,128)S(1)}, f32[2048,256]{1,0:T(8,128)S(1)}, f32[2048,256]{1,...) custom-call(f32[2048,512]{1,0:T(8,128)} %matrix.1), custom_call_target="tpu_custom_call" | custom-call | tf_op jit(solution)/shard_map/sweep/pallas_call | solution.py:531
  68.1 3.0 %final.1 = f32[2048,512]{1,0:T(8,128)} custom-call(f32[2048,256]{1,0:T(8,128)S(1)} %get-tuple-element.12.done, f32[2048,256]{1,0:T(8,128)S(1)} %get-tuple-element.13.lead, f32[2048,256]{1,0:T(8,128)S(1)} %get-tuple-element.14.keep, f32[2048,256]{1,0:T(8,128)S(1)} %get-tuple-element.15.lead_land, f32[2048,256]{1,0:T(8,128)S(1)} %get-tuple-element.16.keep_land, ...), custom_call_target="tpu_custom_call" | custom-call | tf_op jit(solution)/shard_map/final/pallas_call | solution.py:606

commit v10 on v9

--- a/solution.py
+++ b/solution.py
@@ -304,7 +304,7 @@
         multiply(chunk)
 
     def hand_over():
-        loop(0, sent, lambda send: send_lead(send).wait_send())
+        loop(0, sent - 1, lambda send: send_lead(send).wait_send())
 
         @pl.when(signals)
         def _():
@@ -493,6 +493,7 @@
         for copy in lead_copies:
             copy.wait_send()
 
+    send_lead(sent - 1).wait_send()
     for copy in sums + alls + sums_two + alls_two:
         copy.wait_send()
 

time: 71.4 us -> 70.5 us (0.987)
  Pallas kernels: 71.1 us -> 70.2 us
    pallas_call x1, Pallas kernels: 68.1 us -> 67.2 us  [sweep(): pl.pallas_call(functools.partial(sweep_kernel, rows * count, count, lengt...]
where the time goes in v10:
time: 70.5 us; the launch traced here: 70.4 us
  Pallas kernels  70.2 us (100%)
    pallas_call x1, Pallas kernels, sweep(): pl.pallas_call(functools.partial(sweep_kernel, rows * count, count, lengt...  67.2 us
    pallas_call x1, Pallas kernels, final(): pl.pallas_call(functools.partial(final_kernel, lax.axis_size('pairs')), o...  3.02 us

profile of v10, /device:TPU:1, one launch (start us, length us, event | category | flops | bytes accessed | tf_op | source)
XLA Modules:
  0.0 70.4 jit_solution(2760828353553206794)
XLA Ops:
  0.0 67.2 %sweep.1 = (f32[2048,256]{1,0:T(8,128)S(1)}, f32[2048,256]{1,0:T(8,128)S(1)}, f32[2048,256]{1,0:T(8,128)S(1)}, f32[2048,256]{1,0:T(8,128)S(1)}, f32[2048,256]{1,...) custom-call(f32[2048,512]{1,0:T(8,128)} %matrix.1), custom_call_target="tpu_custom_call" | custom-call | tf_op jit(solution)/shard_map/sweep/pallas_call | solution.py:532
  67.2 3.0 %final.1 = f32[2048,512]{1,0:T(8,128)} custom-call(f32[2048,256]{1,0:T(8,128)S(1)} %get-tuple-element.12.done, f32[2048,256]{1,0:T(8,128)S(1)} %get-tuple-element.13.lead, f32[2048,256]{1,0:T(8,128)S(1)} %get-tuple-element.14.keep, f32[2048,256]{1,0:T(8,128)S(1)} %get-tuple-element.15.lead_land, f32[2048,256]{1,0:T(8,128)S(1)} %get-tuple-element.16.keep_land, ...), custom_call_target="tpu_custom_call" | custom-call | tf_op jit(solution)/shard_map/final/pallas_call | solution.py:607
